TPU v7x, 32 devices: a whole 2x2x4 slice. The times are simulated.
32 devices in a mesh: bl: 8 (over y, x, core), bp: 4 (over z).
Axes of the slice: x: 2, y: 2, z: 4, core: 2. Of those that a mesh axis runs over, the one named last changes fastest.
Arguments:
- inverse_cov: float32 [8, 1024, 1024], P('bl', 'bp'), may hold values from -1 to 12, as said below
- channel_keep_mask: int32 [8, 1024], P('bl'), may hold values 0 or 1
- partner_ids: int32 [8, 2], P('bl'), may hold values from -1 to 7, as said below
- band_starts: int32 [2, 64], replicated, may hold values from 0 to 384
Outputs:
- fisher: float32 [2, 64, 64], P(None, 'bp', 'bl')
Inputs may be any that keep to these rules, and one draw needn't show every extreme that they name: partner_ids[i, k] is -1 for an empty slot, else the index of a baseline whose group, its index // 1, lies 1 to 4 groups after the group of baseline i, counted cyclically over the 8 groups; in every draw some baseline has all 2 slots filled. Each inverse_cov[i] is symmetric.
All inputs are finite; a program needn't handle non-finite values. No bound on the sum of `channel_keep_mask` on one device may be relied on, other than what follows from the above.
Results may differ from a plain program's by a relative error of at most 0.0003.
Values sent between devices are 32-bit elements; how exact they have to be, the bound alone decides.
No kernel may reach another device: no remote copies, remote signals or barrier semaphores. Data moves between devices by JAX's collectives and lax.ppermute only.
A program may use at most 128 MiB of HBM per device.

v0:
```python
from functools import partial

import jax
import jax.numpy as jnp
from jax import lax
from jax.sharding import PartitionSpec as P

WINDOW_LENGTH = 128
GROUP_REACH = 4


highest = lax.Precision.HIGHEST


def passed_along(value, axis, steps):
    count = lax.axis_size(axis)
    pairs = [(source, (source + steps) % count) for source in range(count)]
    return lax.ppermute(value, axis, pairs)


def kernel_stack(first_band, band_count, window):
    channel_pos = jnp.arange(window, dtype=jnp.float32)
    spread = jnp.abs(channel_pos[:, None] - channel_pos[None, :])
    band_ids = first_band + jnp.arange(band_count, dtype=jnp.int32)
    length = 1.0 + (band_ids % 4).astype(jnp.float32)
    return jnp.exp(-spread[None, :, :] / length[:, None, None])


def project_turned(panel_block, starts, kernels):
    window = kernels.shape[1]
    window_rows = jax.vmap(
        lambda row_start: lax.dynamic_slice_in_dim(panel_block, row_start, window, 0)
    )(starts)
    return jnp.einsum(
        "apq,aqc->acp", kernels, window_rows, precision=highest, preferred_element_type=jnp.float32
    )


def row_windows(turned, starts, window):

    def one_matrix(matrix):
        return jax.vmap(lambda row_start: lax.dynamic_slice_in_dim(matrix, row_start, window, 0))(
            starts
        )

    return jax.vmap(one_matrix)(turned)


def take_member(received, team_element):
    return lax.dynamic_index_in_dim(received, team_element, 0, keepdims=False)


def contract(turned, block_starts, own_windows):
    partner_windows = row_windows(turned, block_starts, own_windows.shape[2])
    return jnp.einsum(
        "abqp,bapq->ab",
        partner_windows,
        own_windows,
        precision=highest,
        preferred_element_type=jnp.float32,
    )


def block_step(
    block_idx, own_panel, all_start, all_kernels, my_start, projections, presence, block_width
):
    block_begin = block_idx * block_width
    block_starts = lax.dynamic_slice_in_dim(all_start, block_begin, block_width)
    block_kernels = lax.dynamic_slice_in_dim(all_kernels, block_begin, block_width)
    own_turned = project_turned(own_panel, block_starts, block_kernels)
    own_windows = row_windows(own_turned, my_start, all_kernels.shape[1])
    column_sum = jnp.zeros((my_start.shape[0], block_width), jnp.float32)
    for projected, present in zip(projections, presence):
        column_sum = column_sum + lax.cond(
            present,
            partial(contract, projected, block_starts, own_windows),
            partial(jnp.zeros, (my_start.shape[0], block_width), jnp.float32),
        )
    return column_sum


def body(inverse_cov, channel_keep_mask, partner_ids, band_starts):
    local_count, shard_rows, channels = inverse_cov.shape
    panel_width = channels // 2
    window = WINDOW_LENGTH
    band_total = band_starts.shape[1]
    antenna_pair_sets = lax.axis_size("bl")
    owners = lax.axis_size("bp")
    cycle_index = lax.axis_index("bl")
    band_share = band_total // owners
    first_band = lax.axis_index("bp") * band_share
    row_first = lax.axis_index("bp") * shard_rows
    half_start = row_first // panel_width * panel_width
    flag_marks = channel_keep_mask.astype(jnp.float32)
    block_part = lax.dynamic_slice_in_dim(inverse_cov, half_start, panel_width, 2)
    row_marks = lax.dynamic_slice_in_dim(flag_marks, row_first, shard_rows, 1)
    column_marks = lax.dynamic_slice_in_dim(flag_marks, half_start, panel_width, 1)
    masked = block_part * row_marks[:, :, None] * column_marks[:, None, :]
    full_shape = (local_count, 2, panel_width, panel_width)
    own_panels = lax.all_gather(masked, "bp", axis=1, tiled=True).reshape(full_shape)
    arrived = [
        passed_along(own_panels, "bl", -number_of_hops)
        for number_of_hops in range(1, GROUP_REACH + 1)
    ]
    pickers = [partial(take_member, received) for received in arrived]
    my_kernels = kernel_stack(first_band, band_share, window)
    all_kernels = kernel_stack(0, band_total, window)
    block_width = 4
    block_count = band_total // block_width
    halves = [jnp.zeros((band_share, band_total), jnp.float32) for half_index in range(2)]
    targets = partner_ids[0]
    presence_all = targets >= 0
    hop_index = jnp.clip(
        (targets // local_count - cycle_index) % antenna_pair_sets - 1, 0, GROUP_REACH - 1
    )
    team_element = jnp.clip(targets % local_count, 0, local_count - 1)
    summed_panels = jnp.zeros((2, panel_width, panel_width), jnp.float32)
    for slot_index in range(targets.shape[0]):
        summed_panels = summed_panels + jnp.where(
            presence_all[slot_index],
            lax.switch(hop_index[slot_index], pickers, team_element[slot_index]),
            0.0,
        )
    for half_index in range(2):
        all_start = band_starts[half_index]
        my_start = lax.dynamic_slice_in_dim(all_start, first_band, band_share)
        projections = [project_turned(summed_panels[half_index], my_start, my_kernels)]
        presence = [jnp.any(presence_all)]
        stepper = partial(
            block_step,
            own_panel=own_panels[0, half_index],
            all_start=all_start,
            all_kernels=all_kernels,
            my_start=my_start,
            projections=projections,
            presence=presence,
            block_width=block_width,
        )
        block_sums = lax.map(stepper, jnp.arange(block_count, dtype=jnp.int32))
        running_totals = jnp.transpose(block_sums, (1, 0, 2)).reshape(band_share, band_total)
        halves[half_index] = halves[half_index] + running_totals
    normalizer = 1.0 / (4 * local_count * antenna_pair_sets * window)
    partial_fisher = jnp.stack(halves) * normalizer
    return lax.psum_scatter(partial_fisher, "bl", scatter_dimension=2, tiled=True)


def solution(mesh):
    placed = (P("bl", "bp", None), P("bl", None), P("bl", None), P())
    return jax.shard_map(
        body, mesh=mesh, in_specs=placed, out_specs=P(None, "bp", "bl"), check_vma=False
    )
```

profile of v0, /device:TPU:0, one launch (start us, length us, event | category | flops | bytes accessed | tf_op | source)
XLA Modules:
  0.0 1345.1 jit_solution(11537821896451937331)
XLA Ops:
  9.2 48.5 %all-gather.2.cloned.1.call-done = f32[1,1024,512]{2,1,0:T(8,128)} async-done(((f32[1,256,512]{2,1,0:T(8,128)}), f32[1,1024,512]{2,1,0:T(8,128)}) %all-gather.2.cloned.1.call-update) | async-done | bytes 2097168 | tf_op jit(solution)/shard_map/all_gather | solution.py:100
  73.4 32.1 %collective-permute-done = f32[1,2,512,512]{3,2,1,0:T(8,128)} collective-permute-done((f32[1,2,512,512]{3,2,1,0:T(8,128)}, f32[1,2,512,512]{3,2,1,0:T(8,128)}, u32[]{:S(2)}, u32[]{:S(2)}) %collective-permute-start) | collective-permute-done | bytes 2097184 | tf_op jit(solution)/shard_map/ppermute | solution.py:18
  105.5 45.2 %collective-permute-done.1 = f32[1,2,512,512]{3,2,1,0:T(8,128)S(1)} collective-permute-done((f32[1,2,512,512]{3,2,1,0:T(8,128)}, f32[1,2,512,512]{3,2,1,0:T(8,128)S(1)}, u32[]{:S(2)}, u32[]{:S(2)}) %collective-permute-start.1) | collective-permute-done | bytes 2097184 | tf_op jit(solution)/shard_map/ppermute | solution.py:18
  162.5 33.6 %while.30 = (s32[]{:T(128)}, f32[512,512]{1,0:T(8,128)S(1)}, s32[16,2]{0,1:T(2,128)S(1)}, f32[16,128,512]{2,1,0:T(8,128)}, s32[]{:T(128)}) while((s32[]{:T(128)}, f32[512,512]{1,0:T(8,128)S(1)}, s32[16,2]{0,1:T(2,128)S(1)}, f32[16,128,512]{2,1,0:T(8,128)}, s32[]{:T(128)}) %tuple.227), condition=%wide.while_cond.2, body=%wide.while_body.2.sunk | while | flops 2 | bytes 525401 | solution.py:32
  196.1 8.6 fusion.17
  209.1 518.9 %while.27 = (s32[]{:T(128)}, f32[16,16,4]{1,2,0:T(4,128)S(1)}, pred[]{:T(512)}, s32[16]{0:T(128)S(1)}, s32[64]{0:T(128)S(1)}, /*index=5*/f32[512,512]{1,0:T(8,12...) while((s32[]{:T(128)}, f32[16,16,4]{1,2,0:T(4,128)S(1)}, ...), condition=%wide.region_12.13_spmd, body=%wide.region_9.12_spmd.sunk | while | flops 404750400 | bytes 38540844 | solution.py:139
  210.5 8.5 while.32
  222.4 19.3 %conditional.8 = (f32[1,16,4]{1,2,0:T(4,128)S(1)}) conditional(s32[]{:T(128)} %convert_element_type.36, () %tuple.203, (s32[4]{0:T(128)S(1)}, f32[16,512,128]{2,0,1:T(8,128)}, s32[16]{0:T(128)S(1)}, f32[4,512,128]{2,1,0:T(8,128)S(1)}) %tuple.205), branch_computations={%region_10.10_spmd, %region_11.11_spmd} | conditional | flops 2097188 | bytes 35652680 | solution.py:74
  254.8 19.3 %conditional.8 = (f32[1,16,4]{1,2,0:T(4,128)S(1)}) conditional(s32[]{:T(128)} %convert_element_type.36, () %tuple.203, (s32[4]{0:T(128)S(1)}, f32[16,512,128]{2,0,1:T(8,128)}, s32[16]{0:T(128)S(1)}, f32[4,512,128]{2,1,0:T(8,128)S(1)}) %tuple.205), branch_computations={%region_10.10_spmd, %region_11.11_spmd} | conditional | flops 2097188 | bytes 35652680 | solution.py:74
  287.3 19.3 %conditional.8 = (f32[1,16,4]{1,2,0:T(4,128)S(1)}) conditional(s32[]{:T(128)} %convert_element_type.36, () %tuple.203, (s32[4]{0:T(128)S(1)}, f32[16,512,128]{2,0,1:T(8,128)}, s32[16]{0:T(128)S(1)}, f32[4,512,128]{2,1,0:T(8,128)S(1)}) %tuple.205), branch_computations={%region_10.10_spmd, %region_11.11_spmd} | conditional | flops 2097188 | bytes 35652680 | solution.py:74
  307.8 8.5 while.32
  319.7 19.3 %conditional.8 = (f32[1,16,4]{1,2,0:T(4,128)S(1)}) conditional(s32[]{:T(128)} %convert_element_type.36, () %tuple.203, (s32[4]{0:T(128)S(1)}, f32[16,512,128]{2,0,1:T(8,128)}, s32[16]{0:T(128)S(1)}, f32[4,512,128]{2,1,0:T(8,128)S(1)}) %tuple.205), branch_computations={%region_10.10_spmd, %region_11.11_spmd} | conditional | flops 2097188 | bytes 35652680 | solution.py:74
  340.2 8.5 while.32
  352.1 19.3 %conditional.8 = (f32[1,16,4]{1,2,0:T(4,128)S(1)}) conditional(s32[]{:T(128)} %convert_element_type.36, () %tuple.203, (s32[4]{0:T(128)S(1)}, f32[16,512,128]{2,0,1:T(8,128)}, s32[16]{0:T(128)S(1)}, f32[4,512,128]{2,1,0:T(8,128)S(1)}) %tuple.205), branch_computations={%region_10.10_spmd, %region_11.11_spmd} | conditional | flops 2097188 | bytes 35652680 | solution.py:74
  372.6 8.5 while.32
  384.5 19.3 %conditional.8 = (f32[1,16,4]{1,2,0:T(4,128)S(1)}) conditional(s32[]{:T(128)} %convert_element_type.36, () %tuple.203, (s32[4]{0:T(128)S(1)}, f32[16,512,128]{2,0,1:T(8,128)}, s32[16]{0:T(128)S(1)}, f32[4,512,128]{2,1,0:T(8,128)S(1)}) %tuple.205), branch_computations={%region_10.10_spmd, %region_11.11_spmd} | conditional | flops 2097188 | bytes 35652680 | solution.py:74
  405.0 8.5 while.32
  416.9 19.3 %conditional.8 = (f32[1,16,4]{1,2,0:T(4,128)S(1)}) conditional(s32[]{:T(128)} %convert_element_type.36, () %tuple.203, (s32[4]{0:T(128)S(1)}, f32[16,512,128]{2,0,1:T(8,128)}, s32[16]{0:T(128)S(1)}, f32[4,512,128]{2,1,0:T(8,128)S(1)}) %tuple.205), branch_computations={%region_10.10_spmd, %region_11.11_spmd} | conditional | flops 2097188 | bytes 35652680 | solution.py:74
  437.4 8.5 while.32
  449.3 19.3 %conditional.8 = (f32[1,16,4]{1,2,0:T(4,128)S(1)}) conditional(s32[]{:T(128)} %convert_element_type.36, () %tuple.203, (s32[4]{0:T(128)S(1)}, f32[16,512,128]{2,0,1:T(8,128)}, s32[16]{0:T(128)S(1)}, f32[4,512,128]{2,1,0:T(8,128)S(1)}) %tuple.205), branch_computations={%region_10.10_spmd, %region_11.11_spmd} | conditional | flops 2097188 | bytes 35652680 | solution.py:74
  481.8 19.3 %conditional.8 = (f32[1,16,4]{1,2,0:T(4,128)S(1)}) conditional(s32[]{:T(128)} %convert_element_type.36, () %tuple.203, (s32[4]{0:T(128)S(1)}, f32[16,512,128]{2,0,1:T(8,128)}, s32[16]{0:T(128)S(1)}, f32[4,512,128]{2,1,0:T(8,128)S(1)}) %tuple.205), branch_computations={%region_10.10_spmd, %region_11.11_spmd} | conditional | flops 2097188 | bytes 35652680 | solution.py:74
  514.2 19.3 %conditional.8 = (f32[1,16,4]{1,2,0:T(4,128)S(1)}) conditional(s32[]{:T(128)} %convert_element_type.36, () %tuple.203, (s32[4]{0:T(128)S(1)}, f32[16,512,128]{2,0,1:T(8,128)}, s32[16]{0:T(128)S(1)}, f32[4,512,128]{2,1,0:T(8,128)S(1)}) %tuple.205), branch_computations={%region_10.10_spmd, %region_11.11_spmd} | conditional | flops 2097188 | bytes 35652680 | solution.py:74
  546.6 19.3 %conditional.8 = (f32[1,16,4]{1,2,0:T(4,128)S(1)}) conditional(s32[]{:T(128)} %convert_element_type.36, () %tuple.203, (s32[4]{0:T(128)S(1)}, f32[16,512,128]{2,0,1:T(8,128)}, s32[16]{0:T(128)S(1)}, f32[4,512,128]{2,1,0:T(8,128)S(1)}) %tuple.205), branch_computations={%region_10.10_spmd, %region_11.11_spmd} | conditional | flops 2097188 | bytes 35652680 | solution.py:74
  579.0 19.3 %conditional.8 = (f32[1,16,4]{1,2,0:T(4,128)S(1)}) conditional(s32[]{:T(128)} %convert_element_type.36, () %tuple.203, (s32[4]{0:T(128)S(1)}, f32[16,512,128]{2,0,1:T(8,128)}, s32[16]{0:T(128)S(1)}, f32[4,512,128]{2,1,0:T(8,128)S(1)}) %tuple.205), branch_computations={%region_10.10_spmd, %region_11.11_spmd} | conditional | flops 2097188 | bytes 35652680 | solution.py:74
  611.4 19.3 %conditional.8 = (f32[1,16,4]{1,2,0:T(4,128)S(1)}) conditional(s32[]{:T(128)} %convert_element_type.36, () %tuple.203, (s32[4]{0:T(128)S(1)}, f32[16,512,128]{2,0,1:T(8,128)}, s32[16]{0:T(128)S(1)}, f32[4,512,128]{2,1,0:T(8,128)S(1)}) %tuple.205), branch_computations={%region_10.10_spmd, %region_11.11_spmd} | conditional | flops 2097188 | bytes 35652680 | solution.py:74
  643.8 19.3 %conditional.8 = (f32[1,16,4]{1,2,0:T(4,128)S(1)}) conditional(s32[]{:T(128)} %convert_element_type.36, () %tuple.203, (s32[4]{0:T(128)S(1)}, f32[16,512,128]{2,0,1:T(8,128)}, s32[16]{0:T(128)S(1)}, f32[4,512,128]{2,1,0:T(8,128)S(1)}) %tuple.205), branch_computations={%region_10.10_spmd, %region_11.11_spmd} | conditional | flops 2097188 | bytes 35652680 | solution.py:74
  676.3 19.3 %conditional.8 = (f32[1,16,4]{1,2,0:T(4,128)S(1)}) conditional(s32[]{:T(128)} %convert_element_type.36, () %tuple.203, (s32[4]{0:T(128)S(1)}, f32[16,512,128]{2,0,1:T(8,128)}, s32[16]{0:T(128)S(1)}, f32[4,512,128]{2,1,0:T(8,128)S(1)}) %tuple.205), branch_computations={%region_10.10_spmd, %region_11.11_spmd} | conditional | flops 2097188 | bytes 35652680 | solution.py:74
  708.7 19.3 %conditional.8 = (f32[1,16,4]{1,2,0:T(4,128)S(1)}) conditional(s32[]{:T(128)} %convert_element_type.36, () %tuple.203, (s32[4]{0:T(128)S(1)}, f32[16,512,128]{2,0,1:T(8,128)}, s32[16]{0:T(128)S(1)}, f32[4,512,128]{2,1,0:T(8,128)S(1)}) %tuple.205), branch_computations={%region_10.10_spmd, %region_11.11_spmd} | conditional | flops 2097188 | bytes 35652680 | solution.py:74
  730.6 45.0 %while.31 = (s32[]{:T(128)}, f32[512,512]{1,0:T(8,128)}, s32[16,2]{0,1:T(2,128)S(1)}, f32[16,128,512]{2,1,0:T(8,128)}, s32[]{:T(128)}) while((s32[]{:T(128)}, f32[512,512]{1,0:T(8,128)}, s32[16,2]{0,1:T(2,128)S(1)}, f32[16,128,512]{2,1,0:T(8,128)}, s32[]{:T(128)}) %tuple.221), condition=%wide.while_cond.3, body=%wide.while_body.3.sunk | while | flops 2 | bytes 525401 | solution.py:32
  775.6 8.8 fusion.16
  788.8 457.4 %while.29 = (s32[]{:T(128)}, f32[16,16,4]{1,2,0:T(4,128)S(1)}, pred[]{:T(512)}, s32[16]{0:T(128)S(1)}, s32[64]{0:T(128)S(1)}, /*index=5*/f32[512,512]{1,0:T(8,12...) while((s32[]{:T(128)}, f32[16,16,4]{1,2,0:T(4,128)S(1)}, ...), condition=%wide.region_16.17_spmd, body=%wide.region_13.16_spmd.sunk | while | flops 404750400 | bytes 38540844 | solution.py:139
  798.1 19.3 %conditional.9 = (f32[1,16,4]{1,2,0:T(4,128)S(1)}) conditional(s32[]{:T(128)} %convert_element_type.37, () %tuple.208, (s32[4]{0:T(128)S(1)}, f32[16,512,128]{2,0,1:T(8,128)}, s32[16]{0:T(128)S(1)}, f32[4,512,128]{2,1,0:T(8,128)S(1)}) %tuple.210), branch_computations={%region_14.14_spmd, %region_15.15_spmd} | conditional | flops 2097188 | bytes 35652680 | solution.py:74
  826.7 19.3 %conditional.9 = (f32[1,16,4]{1,2,0:T(4,128)S(1)}) conditional(s32[]{:T(128)} %convert_element_type.37, () %tuple.208, (s32[4]{0:T(128)S(1)}, f32[16,512,128]{2,0,1:T(8,128)}, s32[16]{0:T(128)S(1)}, f32[4,512,128]{2,1,0:T(8,128)S(1)}) %tuple.210), branch_computations={%region_14.14_spmd, %region_15.15_spmd} | conditional | flops 2097188 | bytes 35652680 | solution.py:74
  855.3 19.3 %conditional.9 = (f32[1,16,4]{1,2,0:T(4,128)S(1)}) conditional(s32[]{:T(128)} %convert_element_type.37, () %tuple.208, (s32[4]{0:T(128)S(1)}, f32[16,512,128]{2,0,1:T(8,128)}, s32[16]{0:T(128)S(1)}, f32[4,512,128]{2,1,0:T(8,128)S(1)}) %tuple.210), branch_computations={%region_14.14_spmd, %region_15.15_spmd} | conditional | flops 2097188 | bytes 35652680 | solution.py:74
  883.9 19.3 %conditional.9 = (f32[1,16,4]{1,2,0:T(4,128)S(1)}) conditional(s32[]{:T(128)} %convert_element_type.37, () %tuple.208, (s32[4]{0:T(128)S(1)}, f32[16,512,128]{2,0,1:T(8,128)}, s32[16]{0:T(128)S(1)}, f32[4,512,128]{2,1,0:T(8,128)S(1)}) %tuple.210), branch_computations={%region_14.14_spmd, %region_15.15_spmd} | conditional | flops 2097188 | bytes 35652680 | solution.py:74
  912.5 19.3 %conditional.9 = (f32[1,16,4]{1,2,0:T(4,128)S(1)}) conditional(s32[]{:T(128)} %convert_element_type.37, () %tuple.208, (s32[4]{0:T(128)S(1)}, f32[16,512,128]{2,0,1:T(8,128)}, s32[16]{0:T(128)S(1)}, f32[4,512,128]{2,1,0:T(8,128)S(1)}) %tuple.210), branch_computations={%region_14.14_spmd, %region_15.15_spmd} | conditional | flops 2097188 | bytes 35652680 | solution.py:74
  941.1 19.3 %conditional.9 = (f32[1,16,4]{1,2,0:T(4,128)S(1)}) conditional(s32[]{:T(128)} %convert_element_type.37, () %tuple.208, (s32[4]{0:T(128)S(1)}, f32[16,512,128]{2,0,1:T(8,128)}, s32[16]{0:T(128)S(1)}, f32[4,512,128]{2,1,0:T(8,128)S(1)}) %tuple.210), branch_computations={%region_14.14_spmd, %region_15.15_spmd} | conditional | flops 2097188 | bytes 35652680 | solution.py:74
  969.7 19.3 %conditional.9 = (f32[1,16,4]{1,2,0:T(4,128)S(1)}) conditional(s32[]{:T(128)} %convert_element_type.37, () %tuple.208, (s32[4]{0:T(128)S(1)}, f32[16,512,128]{2,0,1:T(8,128)}, s32[16]{0:T(128)S(1)}, f32[4,512,128]{2,1,0:T(8,128)S(1)}) %tuple.210), branch_computations={%region_14.14_spmd, %region_15.15_spmd} | conditional | flops 2097188 | bytes 35652680 | solution.py:74
  998.2 19.3 %conditional.9 = (f32[1,16,4]{1,2,0:T(4,128)S(1)}) conditional(s32[]{:T(128)} %convert_element_type.37, () %tuple.208, (s32[4]{0:T(128)S(1)}, f32[16,512,128]{2,0,1:T(8,128)}, s32[16]{0:T(128)S(1)}, f32[4,512,128]{2,1,0:T(8,128)S(1)}) %tuple.210), branch_computations={%region_14.14_spmd, %region_15.15_spmd} | conditional | flops 2097188 | bytes 35652680 | solution.py:74
  1026.8 19.3 %conditional.9 = (f32[1,16,4]{1,2,0:T(4,128)S(1)}) conditional(s32[]{:T(128)} %convert_element_type.37, () %tuple.208, (s32[4]{0:T(128)S(1)}, f32[16,512,128]{2,0,1:T(8,128)}, s32[16]{0:T(128)S(1)}, f32[4,512,128]{2,1,0:T(8,128)S(1)}) %tuple.210), branch_computations={%region_14.14_spmd, %region_15.15_spmd} | conditional | flops 2097188 | bytes 35652680 | solution.py:74
  1055.4 19.3 %conditional.9 = (f32[1,16,4]{1,2,0:T(4,128)S(1)}) conditional(s32[]{:T(128)} %convert_element_type.37, () %tuple.208, (s32[4]{0:T(128)S(1)}, f32[16,512,128]{2,0,1:T(8,128)}, s32[16]{0:T(128)S(1)}, f32[4,512,128]{2,1,0:T(8,128)S(1)}) %tuple.210), branch_computations={%region_14.14_spmd, %region_15.15_spmd} | conditional | flops 2097188 | bytes 35652680 | solution.py:74
  1084.0 19.3 %conditional.9 = (f32[1,16,4]{1,2,0:T(4,128)S(1)}) conditional(s32[]{:T(128)} %convert_element_type.37, () %tuple.208, (s32[4]{0:T(128)S(1)}, f32[16,512,128]{2,0,1:T(8,128)}, s32[16]{0:T(128)S(1)}, f32[4,512,128]{2,1,0:T(8,128)S(1)}) %tuple.210), branch_computations={%region_14.14_spmd, %region_15.15_spmd} | conditional | flops 2097188 | bytes 35652680 | solution.py:74
  1112.6 19.3 %conditional.9 = (f32[1,16,4]{1,2,0:T(4,128)S(1)}) conditional(s32[]{:T(128)} %convert_element_type.37, () %tuple.208, (s32[4]{0:T(128)S(1)}, f32[16,512,128]{2,0,1:T(8,128)}, s32[16]{0:T(128)S(1)}, f32[4,512,128]{2,1,0:T(8,128)S(1)}) %tuple.210), branch_computations={%region_14.14_spmd, %region_15.15_spmd} | conditional | flops 2097188 | bytes 35652680 | solution.py:74
  1141.2 19.3 %conditional.9 = (f32[1,16,4]{1,2,0:T(4,128)S(1)}) conditional(s32[]{:T(128)} %convert_element_type.37, () %tuple.208, (s32[4]{0:T(128)S(1)}, f32[16,512,128]{2,0,1:T(8,128)}, s32[16]{0:T(128)S(1)}, f32[4,512,128]{2,1,0:T(8,128)S(1)}) %tuple.210), branch_computations={%region_14.14_spmd, %region_15.15_spmd} | conditional | flops 2097188 | bytes 35652680 | solution.py:74
  1169.8 19.3 %conditional.9 = (f32[1,16,4]{1,2,0:T(4,128)S(1)}) conditional(s32[]{:T(128)} %convert_element_type.37, () %tuple.208, (s32[4]{0:T(128)S(1)}, f32[16,512,128]{2,0,1:T(8,128)}, s32[16]{0:T(128)S(1)}, f32[4,512,128]{2,1,0:T(8,128)S(1)}) %tuple.210), branch_computations={%region_14.14_spmd, %region_15.15_spmd} | conditional | flops 2097188 | bytes 35652680 | solution.py:74
  1198.4 19.3 %conditional.9 = (f32[1,16,4]{1,2,0:T(4,128)S(1)}) conditional(s32[]{:T(128)} %convert_element_type.37, () %tuple.208, (s32[4]{0:T(128)S(1)}, f32[16,512,128]{2,0,1:T(8,128)}, s32[16]{0:T(128)S(1)}, f32[4,512,128]{2,1,0:T(8,128)S(1)}) %tuple.210), branch_computations={%region_14.14_spmd, %region_15.15_spmd} | conditional | flops 2097188 | bytes 35652680 | solution.py:74
  1227.0 19.3 %conditional.9 = (f32[1,16,4]{1,2,0:T(4,128)S(1)}) conditional(s32[]{:T(128)} %convert_element_type.37, () %tuple.208, (s32[4]{0:T(128)S(1)}, f32[16,512,128]{2,0,1:T(8,128)}, s32[16]{0:T(128)S(1)}, f32[4,512,128]{2,1,0:T(8,128)S(1)}) %tuple.210), branch_computations={%region_14.14_spmd, %region_15.15_spmd} | conditional | flops 2097188 | bytes 35652680 | solution.py:74
  1246.3 91.1 %all-reduce.8 = f32[2,16,64]{2,1,0:T(8,128)S(1)} all-reduce(f32[2,16,64]{2,1,0:T(8,128)S(1)} %maximum_multiply_fusion), channel_id=2, replica_groups=mesh['bl'=8,'bp'=4] {'bl'}, use_global_device_ids=true, to_apply=%region_17.18.clone | all-reduce | flops 2048 | bytes 16384
  (1002 shorter events, 1213.6 us)
Async XLA Ops:
  6.5 51.2 %all-gather.2.cloned.1.call-start = ((), (), s32[]{:S(2)}) async-start(), calls=%async_computation | async-start | bytes 2621440 | tf_op jit(solution)/shard_map/all_gather | solution.py:100
  57.8 47.8 %collective-permute-start = (f32[1,2,512,512]{3,2,1,0:T(8,128)}, f32[1,2,512,512]{3,2,1,0:T(8,128)}, u32[]{:S(2)}, u32[]{:S(2)}) collective-permute-start(f32[1,2,512,512]{3,2,1,0:T(8,128)} %bitcast.114), channel_id=1, source_target_pairs={{0,28},{4,0},{8,4},{12,8},{16,12},{20,16},{24,20},{28,24},{1,29},{... | collective-permute-start | bytes 6291464 | tf_op jit(solution)/shard_map/ppermute | solution.py:18
  59.4 91.3 %collective-permute-start.1 = (f32[1,2,512,512]{3,2,1,0:T(8,128)}, f32[1,2,512,512]{3,2,1,0:T(8,128)S(1)}, u32[]{:S(2)}, u32[]{:S(2)}) collective-permute-start(f32[1,2,512,512]{3,2,1,0:T(8,128)} %bitcast.115), channel_id=1, source_target_pairs={{0,24},{4,28},{8,0},{12,4},{16,8},{20,12},{24,16},{28,20},{1,25},{... | collective-permute-start | bytes 6291464 | tf_op jit(solution)/shard_map/ppermute | solution.py:18
  60.1 90.8 %collective-permute-start.2 = (f32[1,2,512,512]{3,2,1,0:T(8,128)}, f32[1,2,512,512]{3,2,1,0:T(8,128)}, u32[]{:S(2)}, u32[]{:S(2)}) collective-permute-start(f32[1,2,512,512]{3,2,1,0:T(8,128)} %bitcast.116), channel_id=1, source_target_pairs={{0,20},{4,24},{8,28},{12,0},{16,4},{20,8},{24,12},{28,16},{1,21},{... | collective-permute-start | bytes 6291464 | tf_op jit(solution)/shard_map/ppermute | solution.py:18
  60.5 90.4 %collective-permute-start.3 = (f32[1,2,512,512]{3,2,1,0:T(8,128)}, f32[1,2,512,512]{3,2,1,0:T(8,128)}, u32[]{:S(2)}, u32[]{:S(2)}) collective-permute-start(f32[1,2,512,512]{3,2,1,0:T(8,128)} %bitcast.117), channel_id=1, source_target_pairs={{0,16},{4,20},{8,24},{12,28},{16,0},{20,4},{24,8},{28,12},{1,17},{... | collective-permute-start | bytes 6291464 | tf_op jit(solution)/shard_map/ppermute | solution.py:18
  67.4 4.9 copy-start
Sparse Core Ops, SparseCore 0:
  9.3 48.3 all-gather.1
where the time goes:
time: 1350 us
  local copies, waits for them, and re-layouts  795 us (59%)
  other arithmetic  163 us (12%)
  waiting for transfers between devices  126 us (9%)
  matrix products  106 us (8%)
  blocking collectives  91.1 us (7%)
  loops' own time  44.6 us (3%)
  between operations  15.4 us (1%)
    gather x64, local copies, waits for them, and re-layouts, one_matrix(): lax.dynamic_slice_in_dim(matrix, row_start, window, 0)  309 us
    gather x480, local copies, waits for them, and re-layouts  285 us
    cond x32, other arithmetic  149 us
    cond x34, local copies, waits for them, and re-layouts  138 us
    dot_general x34, matrix products, project_turned(): jnp.einsum('apq,aqc->acp', kernels, window_rows, precision=highest, prefe...  106 us
    unnamed x1, blocking collectives  91.1 us
    ppermute x4, waiting for transfers between devices, passed_along(): return lax.ppermute(value, axis, pairs)  77.5 us
    all_gather x1, waiting for transfers between devices, body(): lax.all_gather(masked, 'bp', axis=1, tiled=True).reshape(full_shape)  48.5 us
  transfers between devices with their start and end apart: 5, of which 4 were waited for; matrix products, arithmetic and copies ran while one was open for 1% of the time, Pallas kernels for 0%

commit v1 on v0

v1 whole, which is shorter than its diff:
```python
from functools import partial

import jax
import jax.numpy as jnp
from jax import lax
from jax.experimental import pallas as pl
from jax.experimental.pallas import tpu as pltpu
from jax.sharding import PartitionSpec as P

WINDOW = 128
KINDS = 4
GROUP_REACH = 4

f32 = jnp.float32
bf16 = jnp.bfloat16
SMEM = pl.BlockSpec(memory_space=pltpu.SMEM)
VMEM = pl.BlockSpec(memory_space=pltpu.VMEM)


def params(mib):
    return pltpu.CompilerParams(vmem_limit_bytes=mib << 20)


def dot(a, b):
    return jnp.dot(a, b, preferred_element_type=f32)


def split(x):
    high = x.astype(bf16)
    return high, (x - high.astype(f32)).astype(bf16)


def left3(x):
    high, low = split(x)
    return jnp.concatenate([high, low, high], axis=1)


def right3(x):
    high, low = split(x)
    return jnp.concatenate([high, high, low], axis=0)


def dot3(a, b):
    return dot(left3(a), right3(b))


def iota(shape, dim):
    return lax.broadcasted_iota(jnp.int32, shape, dim)


def block_place(place, block):
    return jnp.where(place == 0, block, jnp.where(block < 2, block + 2, 3 - block))


def positions(place, count, dim, shape, block):
    index = iota(shape, dim)
    other = index + jnp.where(index < 2 * block, 2, jnp.where(index < 3 * block, -1, -3)) * block
    return jnp.where(place == 0, index, other).astype(f32)


def pack_kernel(sc, pid, cov, keep, panel_out, diag_out, pack_out):
    place, group = sc[1], sc[3]
    rows, width = cov.shape[1], cov.shape[2]
    block = rows // 2
    marks = keep[...].astype(f32)
    half_marks = jnp.where(sc[0] == 0, marks[:, :width], marks[:, width:])
    row_marks = jnp.where(place == 0, half_marks[:, :rows], half_marks[:, rows:])
    row_col = jnp.transpose(jnp.broadcast_to(row_marks, (128, rows)))[:, :1]
    masked = cov[0] * row_col * half_marks
    first = place == 0
    own = jnp.where(first, masked[:, :rows], masked[:, rows:])
    c0 = jnp.where(first, masked[:, 2 * block : 3 * block], masked[:, block : 2 * block])
    c1 = jnp.where(first, masked[:, 3 * block :], masked[:, :block])
    panel_out[:, :rows] = own
    panel_out[:, rows : rows + block] = c0
    panel_out[:, rows + block :] = c1
    d00, d01 = own[:block, :block], own[:block, block:]
    d10, d11 = own[block:, :block], own[block:, block:]
    diag_out[:block, :block] = jnp.where(first, d11, d00)
    diag_out[:block, block:] = jnp.where(first, d10, d01)
    diag_out[block:, :block] = jnp.where(first, d01, d10)
    diag_out[block:, block:] = jnp.where(first, d00, d11)
    above = iota((block, block), 0) < iota((block, block), 1)
    on = iota((block, block), 0) == iota((block, block), 1)
    pack_out[:block] = d01
    pack_out[block : 2 * block] = jnp.where(above, d00, d11)
    pack_out[2 * block : 3 * block] = c0[:block]
    pack_out[3 * block : 4 * block] = c1[block:]
    diag = jnp.sum(jnp.where(on, d00, 0.0), axis=0, keepdims=True)
    slots = pid.shape[1]
    line = iota((8, block), 0)
    extra = jnp.where(line == 0, diag, 0.0)
    extra = jnp.where(line == 1, group.astype(f32), extra)
    for slot in range(slots):
        extra = jnp.where(line == 2 + slot, pid[0, slot].astype(f32), extra)
    pack_out[4 * block :] = extra


def start_rows(sc, starts):
    row = jnp.where(sc[0] == 0, starts[0:1, :], starts[1:2, :]).astype(f32)
    row = jnp.concatenate([row, row], axis=1)
    column = jnp.transpose(jnp.broadcast_to(row, (row.shape[1], row.shape[1])))[:, :1]
    return row, column


def rate(shape, dim):
    return -1.0 / (1 + iota(shape, dim) % KINDS).astype(f32)


def outside(offset, decay, side):
    before = jnp.where(offset < 0, jnp.exp(jnp.minimum(-1.0 - offset, 1e4).clip(0.0) * decay), 0.0)
    past = offset - WINDOW
    after = jnp.where(past >= 0, jnp.exp(past.clip(0.0) * decay), 0.0)
    return jnp.where(side, after, before)


def inside(offset, decay, side):
    held = (offset >= 0) & (offset < WINDOW)
    length = jnp.where(side, WINDOW - offset, offset + 1.0)
    return jnp.where(held, jnp.exp(jnp.where(held, length, 0.0) * decay), 0.0)


def filter_kernel(
    sc, starts, panel, other,
    td_out, to_out, hd_out, h0_out, h1_out, g_out, q_out,
    p3, gd, g0, g1, gr, w3, k3,
):
    place = sc[1]
    rows, width = panel.shape
    block = rows // 2
    bands = 2 * starts.shape[1]
    for at, value in ((slice(0, rows), panel[...]),):
        high, low = split(value)
        p3[0:rows, :] = high
        p3[width : width + rows, :] = high
        p3[2 * width : 2 * width + rows, :] = low
    turned = jnp.transpose(panel[:, rows:])
    high, low = split(turned)
    p3[rows:width, :rows] = high
    p3[width + rows : 2 * width, :rows] = high
    p3[2 * width + rows :, :rows] = low
    high, low = split(other[...])
    p3[rows:width, rows:] = high
    p3[width + rows : 2 * width, rows:] = high
    p3[2 * width + rows :, rows:] = low

    lanes = positions(place, width, 1, (block, width), block)

    def spread_of(index):
        base = block_place(place, index) * block
        return jnp.abs((base + iota((block, width), 0)).astype(f32) - lanes)

    def fill(index, carry):
        spread = spread_of(index)
        at = pl.multiple_of(index * block, block)
        for kind in range(KINDS):
            high, low = split(jnp.exp(spread / -(1.0 + kind)))
            for third, part in enumerate((high, high, low)):
                here = pl.ds(third * width + at, block)
                gd[here, kind * rows : (kind + 1) * rows] = part[:, :rows]
                g0[here, kind * block : (kind + 1) * block] = part[:, rows : rows + block]
                g1[here, kind * block : (kind + 1) * block] = part[:, rows + block :]
        return carry

    lax.fori_loop(0, width // block, fill, 0)

    def fill_rows(index, carry):
        spread = spread_of(index)
        for kind in range(KINDS):
            high, low = split(jnp.exp(spread / -(1.0 + kind)))
            here = pl.ds(pl.multiple_of(kind * rows + index * block, block), block)
            for third, part in enumerate((high, low, high)):
                gr[here, third * width : (third + 1) * width] = part
        return carry

    lax.fori_loop(0, 2, fill_rows, 0)

    row, column = start_rows(sc, starts)
    shape = (width, bands)
    offset = positions(place, width, 0, shape, block) - row
    k3[...] = right3(outside(offset, rate(shape, 1), iota(shape, 1) >= bands // 2))
    shape = (bands, width)
    offset = positions(place, width, 1, shape, block) - column
    weights = outside(offset, rate(shape, 0), iota(shape, 0) >= bands // 2)
    edge3 = left3(dot(left3(weights), p3[...]))
    for kind in range(KINDS):
        at = slice(kind * rows, (kind + 1) * rows)
        hd_out[:, at] = dot(edge3, gd[:, at])
    h0_out[...] = dot(edge3, g0[...])
    h1_out[...] = dot(edge3, g1[...])
    q_out[...] = dot(edge3, k3[...])

    def work(kind, carry):
        at = pl.ds(pl.multiple_of(kind * rows, rows), rows)
        value = dot(gr[at, :], p3[...])
        high, low = split(value)
        w3[:, :width] = high
        w3[:, width : 2 * width] = low
        w3[:, 2 * width :] = high
        for second in range(KINDS):
            here = slice(second * rows, (second + 1) * rows)
            td_out[at, here] = dot(w3[...], gd[:, here])
        for second in range(0, KINDS, 2):
            here = slice(second * block, (second + 2) * block)
            top = pl.ds(pl.multiple_of(kind * rows, block), block)
            low_rows = pl.ds(pl.multiple_of(kind * rows + block, block), block)
            to_out[top, here] = dot(w3[:block, :], g0[:, here])
            to_out[low_rows, here] = dot(w3[block:, :], g1[:, here])
        g_out[at, :] = dot(w3[...], k3[...])
        return carry

    lax.fori_loop(0, KINDS, work, 0)


def dot2(a, b):
    high, low = split(b)
    return dot(a, high) + dot(a, low)


def contract_kernel(
    peer_counts, scale, sc, pid, starts, *refs
):
    count = len(peer_counts)
    packs = refs[:count]
    td, to, hd, h0, h1, g, q, out, m_box, edges, final = refs[count:]
    place, group = sc[1], sc[3]
    rows = td.shape[0] // KINDS
    block = rows // 2
    slots = pid.shape[1]
    half_bands = starts.shape[1]
    bands = 2 * half_bands
    total = extra = None
    for pack, both in zip(packs, peer_counts):
        aux = pack[4 * block :, :]
        source = aux[1:2, :]
        weight = jnp.zeros_like(source)
        for slot in range(slots):
            weight = weight + jnp.where(source == pid[0, slot].astype(f32), 1.0, 0.0)
            if both:
                weight = weight + jnp.where(
                    aux[2 + slot : 3 + slot, :] == group.astype(f32), 1.0, 0.0
                )
        part = pack[: 4 * block, :] * weight
        line = aux[0:1, :] * weight
        total = part if total is None else total + part
        extra = line if extra is None else extra + line
    tri = total[block : 2 * block]
    above = iota((block, block), 0) < iota((block, block), 1)
    on = iota((block, block), 0) == iota((block, block), 1)
    s00 = jnp.where(above, tri, jnp.where(on, 0.5 * extra, 0.0))
    s11 = jnp.where(above, 0.0, jnp.where(on, 0.5 * tri, tri))
    zero = jnp.zeros((block, block), f32)
    s_top = jnp.concatenate([s00, total[:block]], axis=1)
    s_low = jnp.concatenate([zero, s11], axis=1)
    s_own = jnp.concatenate([s_top, s_low], axis=0)
    s_c0 = total[2 * block : 3 * block]
    s_c1 = total[3 * block :]

    row, column = start_rows(sc, starts)
    b_row = row[:, :half_bands]

    def boxes(count, base):
        shape = (KINDS * count, half_bands)
        index = iota(shape, 0)
        kind = index // count
        offset = (base + index % count).astype(f32) - b_row
        hit = (offset >= 0) & (offset < WINDOW) & (iota(shape, 1) % KINDS == kind)
        return jnp.where(hit, 1.0, 0.0).astype(bf16)

    own_base = place * rows
    box_own = boxes(rows, own_base)
    box_c0 = boxes(block, block_place(place, 2) * block)
    box_c1 = boxes(block, block_place(place, 3) * block)

    shape = (bands, rows)
    offset = (own_base + iota(shape, 1)).astype(f32) - column
    reach_rows = inside(offset, rate(shape, 0), iota(shape, 0) >= half_bands)
    shape = (2 * rows, bands)
    offset = positions(place, 2 * rows, 0, shape, block) - row
    reach_cols = inside(offset, rate(shape, 1), iota(shape, 1) >= half_bands)

    v_top = dot3(
        jnp.concatenate([s_top, s_c0], axis=1), reach_cols[: 3 * block]
    )
    v_low = dot3(
        jnp.concatenate([s_low, s_c1], axis=1),
        jnp.concatenate([reach_cols[:rows], reach_cols[3 * block :]], axis=0),
    )
    v = jnp.concatenate([v_top, v_low], axis=0)
    y_own = dot3(reach_rows, s_own)
    y_c0 = dot3(reach_rows[:, :block], s_c0)
    y_c1 = dot3(reach_rows[:, block:], s_c1)

    pair0 = jnp.concatenate([s_c0, s_c0], axis=1)
    pair1 = jnp.concatenate([s_c1, s_c1], axis=1)

    def boxed(x, box):
        high, low = split(x)
        return dot(high, box) + dot(low, box)

    for kind in range(KINDS):
        top, low_rows = kind * rows, kind * rows + block
        at = slice(top, top + rows)
        acc = jnp.zeros((rows, half_bands), f32)
        acc_top = jnp.zeros((block, half_bands), f32)
        acc_low = jnp.zeros((block, half_bands), f32)
        for second in range(KINDS):
            here = slice(second * rows, (second + 1) * rows)
            acc = acc + boxed(s_own * td[at, here], box_own[here])
        for second in range(0, KINDS, 2):
            here = slice(second * block, (second + 2) * block)
            acc_top = acc_top + boxed(pair0 * to[top:low_rows, here], box_c0[here])
            acc_low = acc_low + boxed(pair1 * to[low_rows : top + rows, here], box_c1[here])
        m_box[top:low_rows, :] = acc[:block] + acc_top
        m_box[low_rows : top + rows, :] = acc[block:] + acc_low
        edges[at, :] = v * g[at, :]

    shape = (half_bands, KINDS * rows)
    index = iota(shape, 1)
    offset = (own_base + index % rows).astype(f32) - column[:half_bands]
    hit = (offset >= 0) & (offset < WINDOW) & (iota(shape, 0) % KINDS == index // rows)
    box_rows = jnp.where(hit, 1.0, 0.0).astype(bf16)
    plain = dot2(box_rows, m_box[...])
    third = dot2(box_rows, edges[...])
    second = jnp.zeros((bands, half_bands), f32)
    for kind in range(KINDS):
        here = slice(kind * rows, (kind + 1) * rows)
        second = second + boxed(y_own * hd[:, here], box_own[here])
        here = slice(kind * block, (kind + 1) * block)
        second = second + boxed(y_c0 * h0[:, here], box_c0[here])
        second = second + boxed(y_c1 * h1[:, here], box_c1[here])
    fourth = dot3(reach_rows, v) * q[...]
    third = third - fourth[:half_bands] - fourth[half_bands:]
    result = plain - second[:half_bands] - second[half_bands:]
    result = result - third[:, :half_bands] - third[:, half_bands:]
    final[...] = jnp.zeros(final.shape, f32)
    final[:half_bands, :half_bands] = result
    whole = final[...]
    final[...] = (whole + jnp.transpose(whole)) * scale
    share = out.shape[1]
    owners = out.shape[0] * share // half_bands
    for index in range(out.shape[0]):
        first = index // owners * share
        out[index] = final[first : first + share, :half_bands]


def gather_kernel(owners, sc, parts, out, buffer):
    share, bands = parts.shape[1], parts.shape[2]
    per_half = owners // 2
    buffer[...] = jnp.zeros(buffer.shape, f32)
    for half in range(2):
        acc = None
        for first in range(0, parts.shape[0], owners):
            for place in range(per_half):
                value = parts[first + half * per_half + place]
                acc = value if acc is None else acc + value
        buffer[:share, :bands] = acc
        buffer[...] = jnp.transpose(buffer[...])
        lines = out.shape[1]
        start = pl.multiple_of(sc[2] * lines, 8)
        out[half] = buffer[pl.ds(start, lines), :share]


def partner_routes(groups):
    if groups == 2 * GROUP_REACH:
        routes = []
        for step in (3, 1, 2):

            def target(source, step=step):
                team, member = divmod(source, 2)
                goal = team ^ step
                return goal * 2 + (member if team < goal else 1 - member)

            routes.append(([(source, target(source)) for source in range(groups)], True))
        routes.append(([(source, source ^ 1) for source in range(groups)], False))
        return routes
    return [
        ([(source, (source - hop) % groups) for source in range(groups)], False)
        for hop in range(1, GROUP_REACH + 1)
    ]


def body(inverse_cov, channel_keep_mask, partner_ids, band_starts):
    local_count, rows, channels = inverse_cov.shape
    width = channels // 2
    block = rows // 2
    bands = band_starts.shape[1]
    groups, owners = lax.axis_size("bl"), lax.axis_size("bp")
    per_half = owners // 2
    assert local_count == 1 and width == 2 * rows and block == 128 == 2 * bands
    owner, group = lax.axis_index("bp"), lax.axis_index("bl")
    sc = jnp.stack([owner // per_half, owner % per_half, owner, group]).astype(jnp.int32)
    panel, diag, pack = pl.pallas_call(
        pack_kernel,
        grid_spec=pltpu.PrefetchScalarGridSpec(
            num_scalar_prefetch=2,
            grid=(1,),
            in_specs=[
                pl.BlockSpec((1, rows, width), lambda i, sc, pid: (0, 0, sc[0])),
                pl.BlockSpec((1, channels), lambda i, sc, pid: (0, 0)),
            ],
            out_specs=[
                pl.BlockSpec((rows, width), lambda i, sc, pid: (0, 0)),
                pl.BlockSpec((rows, rows), lambda i, sc, pid: (0, 0)),
                pl.BlockSpec((4 * block + 8, block), lambda i, sc, pid: (0, 0)),
            ],
        ),
        out_shape=[
            jax.ShapeDtypeStruct((rows, width), f32),
            jax.ShapeDtypeStruct((rows, rows), f32),
            jax.ShapeDtypeStruct((4 * block + 8, block), f32),
        ],
        compiler_params=params(16),
    )(sc, partner_ids, inverse_cov, channel_keep_mask)

    other = lax.ppermute(diag, "bp", [(place, place ^ 1) for place in range(owners)])
    routes = partner_routes(groups)
    packs = [lax.ppermute(pack, "bl", route) for route, _ in routes]

    shapes = [
        (KINDS * rows, KINDS * rows),
        (KINDS * rows, KINDS * block),
        (2 * bands, KINDS * rows),
        (2 * bands, KINDS * block),
        (2 * bands, KINDS * block),
        (KINDS * rows, 2 * bands),
        (2 * bands, 2 * bands),
    ]
    tables = pl.pallas_call(
        filter_kernel,
        in_specs=[SMEM, VMEM, VMEM, VMEM],
        out_specs=[VMEM] * 7,
        out_shape=[jax.ShapeDtypeStruct(shape, f32) for shape in shapes],
        scratch_shapes=[
            pltpu.VMEM((3 * width, width), bf16),
            pltpu.VMEM((3 * width, KINDS * rows), bf16),
            pltpu.VMEM((3 * width, KINDS * block), bf16),
            pltpu.VMEM((3 * width, KINDS * block), bf16),
            pltpu.VMEM((KINDS * rows, 3 * width), bf16),
            pltpu.VMEM((rows, 3 * width), bf16),
            pltpu.VMEM((3 * width, 2 * bands), bf16),
        ],
        compiler_params=params(40),
        cost_estimate=pl.CostEstimate(
            flops=9_000_000_000, bytes_accessed=8 << 20, transcendentals=1 << 21
        ),
    )(sc, band_starts, panel, other)

    scale = 1.0 / (4 * local_count * groups * WINDOW)
    share = bands // groups
    parts = pl.pallas_call(
        partial(contract_kernel, [both for _, both in routes], scale),
        in_specs=[SMEM, SMEM, VMEM] + [VMEM] * (len(routes) + 7),
        out_specs=VMEM,
        out_shape=jax.ShapeDtypeStruct((groups * owners, share, bands), f32),
        scratch_shapes=[
            pltpu.VMEM((KINDS * rows, bands), f32),
            pltpu.VMEM((KINDS * rows, 2 * bands), f32),
            pltpu.VMEM((128, 128), f32),
        ],
        compiler_params=params(30),
    )(sc, partner_ids, band_starts, *packs, *tables)

    met = lax.all_to_all(parts, ("bl", "bp"), 0, 0, tiled=True)
    return pl.pallas_call(
        partial(gather_kernel, owners),
        in_specs=[SMEM, VMEM],
        out_specs=VMEM,
        out_shape=jax.ShapeDtypeStruct((2, bands // owners, share), f32),
        scratch_shapes=[pltpu.VMEM((128, 128), f32)],
        compiler_params=params(8),
    )(sc, met)


def solution(mesh):
    placed = (P("bl", "bp", None), P("bl", None), P("bl", None), P())
    return jax.shard_map(
        body, mesh=mesh, in_specs=placed, out_specs=P(None, "bp", "bl"), check_vma=False
    )
```

time: 1350 us -> 47.5 us (0.04)
  local copies, waits for them, and re-layouts: 795 us -> 4.65 us
  other arithmetic: 163 us -> 0.87 us
  waiting for transfers between devices: 126 us -> 3.27 us
  matrix products: 106 us -> 0 us
  blocking collectives: 91.1 us -> 13.3 us
  loops' own time: 44.6 us -> 0 us
  Pallas kernels: 0 us -> 18.9 us
  between operations: 15.4 us -> 0.09 us
    gather x544 -> x0, local copies, waits for them, and re-layouts: 594 us -> none  [the longest x64 309 us: one_matrix(): lax.dynamic_slice_in_dim(matrix, row_start, window, 0)]
    cond x32 -> x0, other arithmetic: 149 us -> none
    cond x34 -> x0, local copies, waits for them, and re-layouts: 138 us -> none
    dot_general x34 -> x0, matrix products: 106 us -> none  [project_turned(): jnp.einsum('apq,aqc->acp', kernels, window_rows, precision=highest, prefe...]
    unnamed x1 -> x0, blocking collectives: 91.1 us -> none
    ppermute x4 -> x5, waiting for transfers between devices: 77.5 us -> 3.27 us  [the longest x1 3.26 us: body(): lax.ppermute(diag, 'bp', [(place, place ^ 1) for place in range(owners)])]
    all_gather x1 -> x0, waiting for transfers between devices: 48.5 us -> none  [body(): lax.all_gather(masked, 'bp', axis=1, tiled=True).reshape(full_shape)]
    another operation x70 -> x0, loops' own time: 44.6 us -> none  [the longest x2 40.8 us: body(): block_sums = lax.map(stepper, jnp.arange(block_count, dtype=jnp.int32))]
  transfers between devices with their start and end apart: 5 -> 5, of which waited for: 4 -> 1; matrix products, arithmetic and copies ran while one was open for 1% -> 0% of each run, Pallas kernels for 0% -> 28%
where the time goes in v1:
time: 47.5 us; the launch traced here: 47.2 us
  Pallas kernels  18.9 us (40%)
  blocking collectives  13.3 us (28%)
  starting transfers between devices  6.16 us (13%)
  local copies, waits for them, and re-layouts  4.65 us (10%)
  waiting for transfers between devices  3.27 us (7%)
  other arithmetic  0.87 us (2%)
    all_to_all x1, blocking collectives, body(): met = lax.all_to_all(parts, ('bl', 'bp'), 0, 0, tiled=True)  13.3 us
    pallas_call x1, Pallas kernels, body(): pl.pallas_call(filter_kernel, in_specs=[SMEM, VMEM, VMEM, VMEM], out_spec...  13.1 us
    pallas_call x1, Pallas kernels, body(): pl.pallas_call(partial(contract_kernel, [both for _, both in routes], sca...  4.22 us
    unnamed x12, local copies, waits for them, and re-layouts  3.47 us
    ppermute x1, waiting for transfers between devices, body(): lax.ppermute(diag, 'bp', [(place, place ^ 1) for place in range(owners)])  3.26 us
    ppermute x1, starting transfers between devices, body(): lax.ppermute(diag, 'bp', [(place, place ^ 1) for place in range(owners)])  3.12 us
    ppermute x4, starting transfers between devices, body(): packs = [lax.ppermute(pack, 'bl', route) for route, _ in routes]  3.04 us
  transfers between devices with their start and end apart: 5, of which 1 were waited for; matrix products, arithmetic and copies ran while one was open for 0% of the time, Pallas kernels for 28%

profile of v1, /device:TPU:0, one launch (start us, length us, event | category | flops | bytes accessed | tf_op | source)
XLA Modules:
  0.0 47.2 jit_solution(2242978043070340039)
XLA Ops:
  0.0 0.1 pad_add_fusion.sc
  0.1 0.0 copy-start
  0.1 1.2 %copy-done = f32[1,256,1024]{2,1,0:T(8,128)S(1)} copy-done((f32[1,256,1024]{2,1,0:T(8,128)S(1)}, f32[1,256,1024]{2,1,0:T(8,128)}, u32[]{:S(2)}) %copy-start) | copy-done | bytes 1048600
  1.3 0.0 copy-start.1
  1.3 0.7 %copy-done.1 = s32[1,1024]{1,0:T(1,128)S(1)} copy-done((s32[1,1024]{1,0:T(1,128)S(1)}, s32[1,1024]{1,0:T(1,128)}, u32[]{:S(2)}) %copy-start.1) | copy-done | bytes 4120
  2.0 0.0 copy-start.2
  2.0 0.7 %copy-done.2 = s32[1,2]{1,0:T(1,128)S(1)} copy-done((s32[1,2]{1,0:T(1,128)S(1)}, s32[1,2]{1,0:T(1,128)}, u32[]{:S(2)}) %copy-start.2) | copy-done | bytes 32
  2.6 0.8 %shard_map.46 = (f32[256,512]{1,0:T(8,128)S(1)}, f32[256,256]{1,0:T(8,128)S(1)}, f32[520,128]{1,0:T(8,128)S(1)}) custom-call(s32[4]{0:T(128)S(1)} %pad_add_fusion.sc, s32[1,2]{1,0:T(1,128)S(1)} %copy-done.2, f32[1,256,1024]{2,1,0:T(8,128)S(1)} %copy-done, s32[1,1024]{1,0:T(1,128)S(1)} %copy-done.1), custom_call_target="tpu_custom_call" | custom-call | tf_op jit(solution)/shard_map/pallas_call | solution.py:393
  3.4 3.1 %collective-permute-start.4 = (f32[256,256]{1,0:T(8,128)S(1)}, f32[256,256]{1,0:T(8,128)S(1)}, u32[]{:S(2)}, u32[]{:S(2)}) collective-permute-start(f32[256,256]{1,0:T(8,128)S(1)} %get-tuple-element.17), channel_id=1, source_target_pairs={{0,1},{1,0},{2,3},{3,2},{4,5},{5,4},{6,7},{7,6},{8,9},{9,8},{10,11... | collective-permute-start | bytes 786440 | tf_op jit(solution)/shard_map/ppermute | solution.py:416
  6.5 2.4 %collective-permute-start = (f32[520,128]{1,0:T(8,128)S(1)}, f32[520,128]{1,0:T(8,128)S(1)}, u32[]{:S(2)}, u32[]{:S(2)}) collective-permute-start(f32[520,128]{1,0:T(8,128)S(1)} %get-tuple-element.15), channel_id=1, source_target_pairs={{0,24},{4,28},{8,16},{12,20},{16,12},{20,8},{24,4},{28,0},{1,25},{... | collective-permute-start | bytes 798728 | tf_op jit(solution)/shard_map/ppermute | solution.py:418
  9.0 0.5 %collective-permute-start.1 = (f32[520,128]{1,0:T(8,128)S(1)}, f32[520,128]{1,0:T(8,128)S(1)}, u32[]{:S(2)}, u32[]{:S(2)}) collective-permute-start(f32[520,128]{1,0:T(8,128)S(1)} %get-tuple-element.15), channel_id=1, source_target_pairs={{0,8},{4,12},{8,4},{12,0},{16,24},{20,28},{24,20},{28,16},{1,9},{5... | collective-permute-start | bytes 798728 | tf_op jit(solution)/shard_map/ppermute | solution.py:418
  9.5 0.0 collective-permute-start.2
  9.6 0.0 collective-permute-start.3
  9.6 3.3 %collective-permute-done.4.other = f32[256,256]{1,0:T(8,128)S(1)} collective-permute-done((f32[256,256]{1,0:T(8,128)S(1)}, f32[256,256]{1,0:T(8,128)S(1)}, u32[]{:S(2)}, u32[]{:S(2)}) %collective-permute-start.4) | collective-permute-done | bytes 262176 | tf_op jit(solution)/shard_map/ppermute | solution.py:416
  12.8 0.0 copy-start.4
  12.8 0.7 %copy-done.4 = s32[2,64]{1,0:T(2,128)S(1)} copy-done((s32[2,64]{1,0:T(2,128)S(1)}, s32[2,64]{1,0:T(2,128)}, u32[]{:S(2)}) %copy-start.4) | copy-done | bytes 536
  13.5 0.0 copy-start.3
  13.5 13.1 %shard_map.47 = (f32[1024,1024]{1,0:T(8,128)S(1)}, f32[1024,512]{1,0:T(8,128)S(1)}, f32[128,1024]{1,0:T(8,128)S(1)}, f32[128,512]{1,0:T(8,128)S(1)}, f32[128,512...) custom-call(s32[4]{0:T(128)S(1)} %pad_add_fusion.sc, s32[2,64]{1,0:T(2,128)S(1)} %copy-done.4, ...), custom_call_target="tpu_custom_call" | custom-call | flops 8999999488 | bytes 8388608 | tf_op jit(solution)/shard_map/pallas_call | solution.py:429
  26.7 0.0 collective-permute-done.refs_0_
  26.7 0.0 collective-permute-done.1.refs_1_
  26.7 0.0 collective-permute-done.2.refs_2_
  26.7 0.0 collective-permute-done.3.refs_3_
  26.7 0.0 copy-done.3
  26.7 4.2 %shard_map.48 = f32[32,8,64]{2,1,0:T(8,128)S(1)} custom-call(s32[4]{0:T(128)S(1)} %pad_add_fusion.sc, s32[1,2]{1,0:T(1,128)S(1)} %copy-done.3, s32[2,64]{1,0:T(2,128)S(1)} %copy-done.4, f32[520,128]{1,0:T(8,128)S(1)} %collective-permute-done.refs_0_, f32[520,128]{1,0:T(8,128)S(1)} %collective-permute-done.1.refs_1_, ...), custom_call_target="tpu_custom_call" | custom-call | tf_op jit(solution)/shard_map/pallas_call | solution.py:451
  30.9 0.1 reshape
  31.1 13.3 %all_to_all.5 = f32[32,1,512]{2,1,0:T(1,128)S(1)} all-to-all(f32[32,1,512]{2,1,0:T(1,128)S(1)} %reshape), channel_id=1, replica_groups=mesh['bl'=8,'bp'=4] {'bl','bp'}, dimensions={0} | all-to-all | bytes 131072 | tf_op jit(solution)/shard_map/all_to_all | solution.py:464
  44.4 0.5 %broadcast.2 = f32[]{:T(128)} broadcast(f32[]{:T(128)} %constant.37), dimensions={} | broadcast | bytes 8 | tf_op jit(solution)/shard_map/all_to_all | solution.py:464
  44.9 0.8 %reduce = f32[32,512]{1,0:T(8,128)S(1)} reduce(f32[32,1,512]{2,1,0:T(1,128)S(1)} %all_to_all.5, f32[]{:T(128)} %broadcast.2), dimensions={1}, to_apply=%all_to_all.3.reduce_sub_computation | reduce | bytes 131076 | tf_op jit(solution)/shard_map/all_to_all | solution.py:464
  45.7 0.1 reshape.1.parts
  45.8 0.8 %shard_map.49 = f32[2,16,8]{2,1,0:T(8,128)S(1)} custom-call(s32[4]{0:T(128)S(1)} %pad_add_fusion.sc, f32[32,8,64]{2,1,0:T(8,128)S(1)} %reshape.1.parts), custom_call_target="tpu_custom_call" | custom-call | tf_op jit(solution)/shard_map/pallas_call | solution.py:465
  46.6 0.7 %copy.5 = f32[2,16,8]{1,2,0:T(8,128)} copy(f32[2,16,8]{2,1,0:T(8,128)S(1)} %shard_map.49) | data formatting | bytes 2048 | tf_op jit(solution)/shard_map/pallas_call | solution.py:465
Async XLA Ops:
  0.1 1.2 %copy-start = (f32[1,256,1024]{2,1,0:T(8,128)S(1)}, f32[1,256,1024]{2,1,0:T(8,128)}, u32[]{:S(2)}) copy-start(f32[1,256,1024]{2,1,0:T(8,128)} %cov.1) | copy-start | bytes 3145732
  1.3 0.7 %copy-start.1 = (s32[1,1024]{1,0:T(1,128)S(1)}, s32[1,1024]{1,0:T(1,128)}, u32[]{:S(2)}) copy-start(s32[1,1024]{1,0:T(1,128)} %keep.1) | copy-start | bytes 12292
  2.0 0.7 %copy-start.2 = (s32[1,2]{1,0:T(1,128)S(1)}, s32[1,2]{1,0:T(1,128)}, u32[]{:S(2)}) copy-start(s32[1,2]{1,0:T(1,128)} %pid.3) | copy-start | bytes 28
  3.4 9.4 %collective-permute-start.4 = (f32[256,256]{1,0:T(8,128)S(1)}, f32[256,256]{1,0:T(8,128)S(1)}, u32[]{:S(2)}, u32[]{:S(2)}) collective-permute-start(f32[256,256]{1,0:T(8,128)S(1)} %get-tuple-element.17), channel_id=1, source_target_pairs={{0,1},{1,0},{2,3},{3,2},{4,5},{5,4},{6,7},{7,6},{8,9},{9,8},{10,11... | collective-permute-start | bytes 786440 | tf_op jit(solution)/shard_map/ppermute | solution.py:416
  6.5 20.1 %collective-permute-start = (f32[520,128]{1,0:T(8,128)S(1)}, f32[520,128]{1,0:T(8,128)S(1)}, u32[]{:S(2)}, u32[]{:S(2)}) collective-permute-start(f32[520,128]{1,0:T(8,128)S(1)} %get-tuple-element.15), channel_id=1, source_target_pairs={{0,24},{4,28},{8,16},{12,20},{16,12},{20,8},{24,4},{28,0},{1,25},{... | collective-permute-start | bytes 798728 | tf_op jit(solution)/shard_map/ppermute | solution.py:418
  9.0 17.7 %collective-permute-start.1 = (f32[520,128]{1,0:T(8,128)S(1)}, f32[520,128]{1,0:T(8,128)S(1)}, u32[]{:S(2)}, u32[]{:S(2)}) collective-permute-start(f32[520,128]{1,0:T(8,128)S(1)} %get-tuple-element.15), channel_id=1, source_target_pairs={{0,8},{4,12},{8,4},{12,0},{16,24},{20,28},{24,20},{28,16},{1,9},{5... | collective-permute-start | bytes 798728 | tf_op jit(solution)/shard_map/ppermute | solution.py:418
  9.5 17.2 %collective-permute-start.2 = (f32[520,128]{1,0:T(8,128)S(1)}, f32[520,128]{1,0:T(8,128)S(1)}, u32[]{:S(2)}, u32[]{:S(2)}) collective-permute-start(f32[520,128]{1,0:T(8,128)S(1)} %get-tuple-element.15), channel_id=1, source_target_pairs={{0,16},{4,20},{8,24},{12,28},{16,4},{20,0},{24,12},{28,8},{1,17},{... | collective-permute-start | bytes 798728 | tf_op jit(solution)/shard_map/ppermute | solution.py:418
  9.6 17.1 %collective-permute-start.3 = (f32[520,128]{1,0:T(8,128)S(1)}, f32[520,128]{1,0:T(8,128)S(1)}, u32[]{:S(2)}, u32[]{:S(2)}) collective-permute-start(f32[520,128]{1,0:T(8,128)S(1)} %get-tuple-element.15), channel_id=1, source_target_pairs={{0,4},{4,0},{8,12},{12,8},{16,20},{20,16},{24,28},{28,24},{1,5},{5... | collective-permute-start | bytes 798728 | tf_op jit(solution)/shard_map/ppermute | solution.py:418
  12.8 0.7 %copy-start.4 = (s32[2,64]{1,0:T(2,128)S(1)}, s32[2,64]{1,0:T(2,128)}, u32[]{:S(2)}) copy-start(s32[2,64]{1,0:T(2,128)} %starts.3) | copy-start | bytes 1540
  13.5 13.2 %copy-start.3 = (s32[1,2]{1,0:T(1,128)S(1)}, s32[1,2]{1,0:T(1,128)}, u32[]{:S(2)}) copy-start(s32[1,2]{1,0:T(1,128)} %pid.3) | copy-start | bytes 28

commit v2 on v1

v2 whole, which is shorter than its diff:
```python
from functools import partial

import jax
import jax.numpy as jnp
from jax import lax
from jax.experimental import pallas as pl
from jax.experimental.pallas import tpu as pltpu
from jax.sharding import PartitionSpec as P

WINDOW = 128
KINDS = 4
GROUP_REACH = 4

f32 = jnp.float32
bf16 = jnp.bfloat16
SMEM = pl.BlockSpec(memory_space=pltpu.SMEM)
VMEM = pl.BlockSpec(memory_space=pltpu.VMEM)
HBM = pl.BlockSpec(memory_space=pltpu.HBM)


def params(mib):
    return pltpu.CompilerParams(vmem_limit_bytes=mib << 20)


def dot(a, b):
    return jnp.dot(a, b, preferred_element_type=f32)


def split(x):
    high = x.astype(bf16)
    return high, (x - high.astype(f32)).astype(bf16)


def left3(x):
    high, low = split(x)
    return jnp.concatenate([high, low, high], axis=1)


def right3(x):
    high, low = split(x)
    return jnp.concatenate([high, high, low], axis=0)


def dot_t(a, b):
    return lax.dot_general(a, b, (((1,), (1,)), ((), ())), preferred_element_type=f32)


def iota(shape, dim):
    return lax.broadcasted_iota(jnp.int32, shape, dim)


def pack_kernel(
    sc, cov_hbm, keep_hbm, pid_hbm, starts_hbm, panel_out, diag_out, pack_out, info_out,
    cov, keep, pid, starts, sems,
):
    rows, width = cov.shape
    columns = pl.ds(pl.multiple_of(sc[0] * width, width), width)
    copies = [
        pltpu.make_async_copy(cov_hbm.at[0, :, columns], cov, sems.at[0]),
        pltpu.make_async_copy(keep_hbm, keep, sems.at[1]),
        pltpu.make_async_copy(pid_hbm, pid, sems.at[2]),
        pltpu.make_async_copy(starts_hbm, starts, sems.at[3]),
    ]
    for copy in copies:
        copy.start()
    for copy in copies:
        copy.wait()
    block = rows // 2
    first = sc[1] == 0
    marks = keep[...].astype(f32)
    half_marks = jnp.where(sc[0] == 0, marks[:, :width], marks[:, width:])
    row_marks = jnp.where(first, half_marks[:, :rows], half_marks[:, rows:])
    row_col = jnp.transpose(jnp.broadcast_to(row_marks, (128, rows)))[:, :1]
    masked = cov[...] * row_col * half_marks
    own = jnp.where(first, masked[:, :rows], masked[:, rows:])
    c0 = jnp.where(first, masked[:, 2 * block : 3 * block], masked[:, block : 2 * block])
    c1 = jnp.where(first, masked[:, 3 * block :], masked[:, :block])
    panel_out[:, :rows] = own
    panel_out[:, rows : rows + block] = c0
    panel_out[:, rows + block :] = c1
    d00, d01 = own[:block, :block], own[:block, block:]
    d10, d11 = own[block:, :block], own[block:, block:]
    diag_out[:block, :block] = jnp.where(first, d11, d00)
    diag_out[:block, block:] = jnp.where(first, d10, d01)
    diag_out[block:, :block] = jnp.where(first, d01, d10)
    diag_out[block:, block:] = jnp.where(first, d00, d11)
    above = iota((block, block), 0) < iota((block, block), 1)
    on = iota((block, block), 0) == iota((block, block), 1)
    pack_out[:block] = d01
    pack_out[block : 2 * block] = jnp.where(above, d00, d11)
    pack_out[2 * block : 3 * block] = c0[:block]
    pack_out[3 * block : 4 * block] = c1[block:]
    line = iota((8, block), 0)
    info = jnp.where(line == 0, jnp.sum(jnp.where(on, d00, 0.0), axis=0, keepdims=True), 0.0)
    info = jnp.where(line == 1, sc[3].astype(f32), info)
    for slot in range(pid.shape[1]):
        info = jnp.where(line == 2 + slot, pid[0, slot].astype(f32), info)
    begin = jnp.where(sc[0] == 0, starts[0:1, :], starts[1:2, :]).astype(f32)
    info = jnp.where(line == 7, jnp.concatenate([begin, begin], axis=1), info)
    pack_out[4 * block :] = info
    info_out[...] = info


def turn(x):
    return jnp.transpose(x)


def decay(shape, dim):
    return -1.0 / (1 + iota(shape, dim) % KINDS).astype(f32)


def held(offset):
    return (offset >= 0) & (offset < WINDOW)


def filter_kernel(
    sc, info, panel, other,
    td_out, to_out, hd_out, h0_out, h1_out, q_out,
    bd_out, b0_out, b1_out, br_out, rh_out, rl_out,
    p3, kr, kc0, kc1, kl,
):
    first = sc[1] == 0
    rows, width = panel.shape
    block = rows // 2
    twice = info.shape[1]
    bands = twice // 2

    high, low = split(panel[...])
    p3[0:rows, :] = high
    p3[rows : 2 * rows, :] = high
    p3[2 * rows : 3 * rows, :] = low
    high, low = split(turn(panel[:, rows:]))
    p3[3 * rows : 4 * rows, :rows] = high
    p3[4 * rows : 5 * rows, :rows] = high
    p3[5 * rows :, :rows] = low
    high, low = split(other[...])
    p3[3 * rows : 4 * rows, rows:] = high
    p3[4 * rows : 5 * rows, rows:] = high
    p3[5 * rows :, rows:] = low

    for chunk in range(2):
        shape = (block, rows)
        line = iota(shape, 0) + chunk * block
        lane = iota(shape, 1)
        spread = jnp.abs(line - lane).astype(f32)
        swapped = jnp.abs((line + block) % rows - (lane + block) % rows).astype(f32)
        cross = jnp.where(first, spread, swapped)
        here = chunk * block
        for kind in range(KINDS):
            at = slice(kind * rows, (kind + 1) * rows)
            high, low = split(jnp.exp(spread / -(1.0 + kind)))
            for third, part in enumerate((high, high, low)):
                kr[third * rows + here : third * rows + here + block, at] = part
            for third, part in enumerate((high, low, high)):
                kl[kind * rows + here : kind * rows + here + block,
                   third * rows : (third + 1) * rows] = part
            high, low = split(jnp.exp(cross / -(1.0 + kind)))
            at = slice(kind * block, (kind + 1) * block)
            for third, part in enumerate((high, high, low)):
                kc0[third * rows + here : third * rows + here + block, at] = part[:, :block]
                kc1[third * rows + here : third * rows + here + block, at] = part[:, block:]

    def own_place(index):
        return index + jnp.where(first, 0, rows)

    def other_place(index):
        return jnp.where(first, index + rows, (index + block) % rows)

    def gap(place):
        return jnp.abs(place.astype(f32) - (rows - 0.5))

    shape = (rows, twice)
    own_column = jnp.exp(gap(own_place(iota(shape, 0))) * decay(shape, 1))
    other_column = jnp.exp(gap(other_place(iota(shape, 0))) * decay(shape, 1))
    shape = (8, rows)
    own_row = jnp.exp(gap(own_place(iota(shape, 1))) * decay(shape, 0))
    other_row = jnp.exp(gap(other_place(iota(shape, 1))) * decay(shape, 0))

    begin = info[7:8, :]
    begin_column = turn(jnp.broadcast_to(begin, (twice, twice)))[:, :1]

    extra = 16
    shape = (twice, rows)
    after = iota(shape, 0) >= bands

    def outside(place):
        offset = place.astype(f32) - begin_column
        reach = jnp.where(after, offset - WINDOW, -1.0 - offset)
        return jnp.where(
            reach >= 0, jnp.exp(jnp.where(reach >= 0, reach, 0.0) * decay(shape, 0)), 0.0
        )

    def inside(place):
        offset = place.astype(f32) - begin_column
        reach = jnp.where(after, WINDOW - offset, offset + 1.0)
        return jnp.where(
            held(offset), jnp.exp(jnp.where(held(offset), reach, 0.0) * decay(shape, 0)), 0.0
        )

    none = jnp.zeros((8, rows), f32)
    four = iota((8, rows), 0) < KINDS
    out_own = outside(own_place(iota(shape, 1)))
    out_other = outside(other_place(iota(shape, 1)))
    weights_own = jnp.concatenate([out_own, jnp.where(four, 0.0, own_row), none], axis=0)
    weights_other = jnp.concatenate([out_other, jnp.where(four, other_row, 0.0), none], axis=0)
    lhs = jnp.concatenate([left3(weights_own), left3(weights_other)], axis=1)
    edge = dot(lhs, p3[...])
    edge_own = left3(edge[:, :rows])
    edge_other = left3(edge[:, rows:])
    from_other = dot(edge_other, right3(other_column))
    from_own = dot(edge_own, right3(own_column))
    near = jnp.concatenate([left3(edge[:twice, :rows]), left3(edge[:twice, rows:])], axis=1)
    flip_own, flip_own_low = split(out_own)
    flip_other, flip_other_low = split(out_other)
    q_out[...] = dot_t(
        near,
        jnp.concatenate(
            [flip_own, flip_own, flip_own_low, flip_other, flip_other, flip_other_low], axis=1
        ),
    )
    for kind in range(KINDS):
        at = slice(kind * rows, (kind + 1) * rows)
        full = dot(edge_own, kr[:, at]) + from_other[:, kind : kind + 1] * own_row[kind : kind + 1]
        hd_out[:, at] = full[:twice]
        turned = turn(full[twice : twice + 8])
        value = dot(kl[at, :], p3[: 3 * rows, :])
        value = value + own_column[:, kind : kind + 1] * edge[twice + kind : twice + kind + 1, :]
        left_own = left3(value[:, :rows])
        left_other = left3(value[:, rows:])
        for second in range(kind, KINDS):
            here = slice(second * rows, (second + 1) * rows)
            to = pair_index(kind, second) * rows
            td_out[to : to + rows, :] = (
                dot(left_own, kr[:, here])
                + turned[:, second : second + 1] * own_row[second : second + 1]
            )
        top = dot(left_other[:block], kc0[...])
        bottom = dot(left_other[block:], kc1[...])
        for second in range(KINDS):
            here = slice(second * block, (second + 1) * block)
            column = turned[:, KINDS + second : KINDS + second + 1]
            line = other_row[second : second + 1]
            to_out[kind * rows : kind * rows + block, here] = (
                top[:, here] + column[:block] * line[:, :block]
            )
            to_out[kind * rows + block : (kind + 1) * rows, here] = (
                bottom[:, here] + column[block:] * line[:, block:]
            )
    high0 = dot(edge_other[:twice], kc0[...])
    high1 = dot(edge_other[:twice], kc1[...])
    for kind in range(KINDS):
        here = slice(kind * block, (kind + 1) * block)
        column = from_own[:twice, kind : kind + 1]
        line = other_row[kind : kind + 1]
        h0_out[:, here] = high0[:, here] + column * line[:, :block]
        h1_out[:, here] = high1[:, here] + column * line[:, block:]

    begins = begin[:, :bands]

    def boxes(count, place):
        shape = (KINDS * count, bands)
        index = iota(shape, 0)
        hit = held(place(index % count).astype(f32) - begins)
        hit = hit & (iota(shape, 1) % KINDS == index // count)
        return jnp.where(hit, 1.0, 0.0).astype(bf16)

    bd_out[...] = boxes(rows, own_place)
    b0_out[...] = boxes(block, other_place)
    b1_out[...] = boxes(block, lambda index: other_place(index + block))
    shape2 = (bands, KINDS * rows)
    index = iota(shape2, 1)
    hit = held(own_place(index % rows).astype(f32) - begin_column[:bands])
    hit = hit & (iota(shape2, 0) % KINDS == index // rows)
    br_out[...] = jnp.where(hit, 1.0, 0.0).astype(bf16)
    high, low = split(inside(own_place(iota(shape, 1))))
    rh_out[:, :rows] = high
    rl_out[:, :rows] = low
    high, low = split(inside(other_place(iota(shape, 1))))
    rh_out[:, rows:] = high
    rl_out[:, rows:] = low


def pair_index(kind, second):
    return kind * KINDS - kind * (kind - 1) // 2 + second - kind


def contract_kernel(peer_counts, slots, scale, owners, info, *refs):
    count = len(peer_counts)
    packs = refs[:count]
    td, to, hd, h0, h1, q, bd, b0, b1, br, rh, rl, out, m_box, final = refs[count:]
    rows = td.shape[1]
    block = rows // 2
    bands = bd.shape[1]
    twice = 2 * bands
    own = info[...]
    total = extra = None
    for pack, both in zip(packs, peer_counts):
        aux = pack[4 * block :, :]
        weight = jnp.zeros_like(aux[:1])
        for slot in range(slots):
            at = slice(2 + slot, 3 + slot)
            weight = weight + jnp.where(aux[1:2] == own[at], 1.0, 0.0)
            if both:
                weight = weight + jnp.where(aux[at] == own[1:2], 1.0, 0.0)
        part = pack[: 4 * block, :] * weight
        line = aux[0:1, :] * weight
        total = part if total is None else total + part
        extra = line if extra is None else extra + line
    upper = total[:block]
    tri = total[block : 2 * block]
    flipped = turn(tri)
    above = iota((block, block), 0) < iota((block, block), 1)
    on = iota((block, block), 0) == iota((block, block), 1)
    s00 = jnp.where(above, tri, jnp.where(on, extra, flipped))
    s11 = jnp.where(above, flipped, tri)
    s_own = jnp.concatenate(
        [
            jnp.concatenate([s00, upper], axis=1),
            jnp.concatenate([turn(upper), s11], axis=1),
        ],
        axis=0,
    )
    s_c0 = total[2 * block : 3 * block]
    s_c1 = total[3 * block :]
    half_own = 0.5 * s_own
    pair0 = jnp.concatenate([s_c0, s_c0], axis=1)
    pair1 = jnp.concatenate([s_c1, s_c1], axis=1)

    def boxed(x, box):
        high, low = split(x)
        return dot(high, box) + dot(low, box)

    for kind in range(KINDS):
        top, mid, end = kind * rows, kind * rows + block, (kind + 1) * rows
        acc = jnp.zeros((rows, bands), f32)
        acc_top = jnp.zeros((block, bands), f32)
        acc_low = jnp.zeros((block, bands), f32)
        for second in range(kind, KINDS):
            here = slice(second * rows, (second + 1) * rows)
            at = pair_index(kind, second) * rows
            value = half_own if second == kind else s_own
            acc = acc + boxed(value * td[at : at + rows, :], bd[here, :])
        for second in range(0, KINDS, 2):
            here = slice(second * block, (second + 2) * block)
            acc_top = acc_top + boxed(pair0 * to[top:mid, here], b0[here, :])
            acc_low = acc_low + boxed(pair1 * to[mid:end, here], b1[here, :])
        m_box[top:mid, :] = acc[:block] + acc_top
        m_box[mid:end, :] = acc[block:] + acc_low
    high, low = split(m_box[...])
    result = dot(br[...], high) + dot(br[...], low)

    reach = (rh[:, :rows], rl[:, :rows])
    reach0 = (rh[:, :block], rl[:, :block])
    reach1 = (rh[:, block:rows], rl[:, block:rows])
    over0 = (rh[:, rows : rows + block], rl[:, rows : rows + block])
    over1 = (rh[:, rows + block :], rl[:, rows + block :])

    def three(a, b, multiply):
        return multiply(a[0], b[0]) + multiply(a[0], b[1]) + multiply(a[1], b[0])

    part_own, part0, part1 = split(s_own), split(s_c0), split(s_c1)
    y_own = three(reach, part_own, dot)
    y_off = jnp.concatenate([three(over0, part0, dot_t), three(over1, part1, dot_t)], axis=1)
    y_0 = three(reach0, part0, dot)
    y_1 = three(reach1, part1, dot)
    fourth = three(split(0.5 * y_own + y_off), reach, dot_t) * q[...]
    y_own = y_own + y_off
    second = jnp.zeros((twice, bands), f32)
    for kind in range(KINDS):
        here = slice(kind * rows, (kind + 1) * rows)
        second = second + boxed(y_own * hd[:, here], bd[here, :])
        here = slice(kind * block, (kind + 1) * block)
        second = second + boxed(y_0 * h0[:, here], b0[here, :])
        second = second + boxed(y_1 * h1[:, here], b1[here, :])
    fourth = fourth[:bands] + fourth[bands:]
    result = result - second[:bands] - second[bands:] + fourth[:, :bands] + fourth[:, bands:]
    final[...] = jnp.zeros(final.shape, f32)
    final[:bands, :bands] = result
    whole = final[...]
    final[...] = (whole + turn(whole)) * scale

    groups = out.shape[0] // owners
    share, lines = bands // groups, bands // owners
    lane = iota((groups, final.shape[1]), 1)
    for owner in range(owners):
        row = jnp.zeros((groups, final.shape[1]), f32)
        for member in range(share):
            value = final[pl.ds(member, groups, stride=share), :]
            move = (member - owner) * lines % final.shape[1]
            value = pltpu.roll(value, move, 1) if move else value
            row = jnp.where(lane // lines == member, value, row)
        for group in range(groups):
            out[group * owners + owner] = row[group : group + 1]


def gather_kernel(owners, parts, out):
    per_half = owners // 2
    lines, share = out.shape[1], out.shape[2]
    lanes = parts.shape[2]
    for half in range(2):
        acc = None
        for first in range(0, parts.shape[0], owners):
            for place in range(per_half):
                value = parts[first + half * per_half + place]
                acc = value if acc is None else acc + value
        line = iota((lanes, lanes), 0)
        table = jnp.zeros((lanes, lanes), f32)
        for member in range(share):
            value = pltpu.roll(acc, (-member * lines) % lanes, 1) if member else acc
            table = jnp.where(line == member, value, table)
        out[half] = turn(table)[:lines, :share]


def partner_routes(groups):
    if groups == 2 * GROUP_REACH:
        routes = []
        for step in (3, 1, 2):

            def target(source, step=step):
                team, member = divmod(source, 2)
                goal = team ^ step
                return goal * 2 + (member if team < goal else 1 - member)

            routes.append(([(source, target(source)) for source in range(groups)], True))
        routes.append(([(source, source ^ 1) for source in range(groups)], False))
        return routes
    return [
        ([(source, (source - hop) % groups) for source in range(groups)], False)
        for hop in range(1, GROUP_REACH + 1)
    ]


def body(inverse_cov, channel_keep_mask, partner_ids, band_starts):
    local_count, rows, channels = inverse_cov.shape
    width = channels // 2
    block = rows // 2
    bands = band_starts.shape[1]
    twice = 2 * bands
    groups, owners = lax.axis_size("bl"), lax.axis_size("bp")
    per_half = owners // 2
    assert local_count == 1 and width == 2 * rows and block == 128 == twice
    owner, group = lax.axis_index("bp"), lax.axis_index("bl")
    sc = jnp.stack([owner // per_half, owner % per_half, owner, group]).astype(jnp.int32)
    panel, diag, pack, info = pl.pallas_call(
        pack_kernel,
        in_specs=[SMEM, HBM, HBM, HBM, HBM],
        out_specs=[VMEM] * 4,
        out_shape=[
            jax.ShapeDtypeStruct((rows, width), f32),
            jax.ShapeDtypeStruct((rows, rows), f32),
            jax.ShapeDtypeStruct((4 * block + 8, block), f32),
            jax.ShapeDtypeStruct((8, block), f32),
        ],
        scratch_shapes=[
            pltpu.VMEM((rows, width), f32),
            pltpu.VMEM((1, channels), jnp.int32),
            pltpu.SMEM(partner_ids.shape, jnp.int32),
            pltpu.VMEM(band_starts.shape, jnp.int32),
            pltpu.SemaphoreType.DMA((4,)),
        ],
        compiler_params=params(16),
    )(sc, inverse_cov, channel_keep_mask, partner_ids, band_starts)

    other = lax.ppermute(diag, "bp", [(place, place ^ 1) for place in range(owners)])
    routes = partner_routes(groups)
    packs = [lax.ppermute(pack, "bl", route) for route, _ in routes]

    pairs = KINDS * (KINDS + 1) // 2
    shapes = [
        ((pairs * rows, rows), f32),
        ((KINDS * rows, KINDS * block), f32),
        ((twice, KINDS * rows), f32),
        ((twice, KINDS * block), f32),
        ((twice, KINDS * block), f32),
        ((twice, twice), f32),
        ((KINDS * rows, bands), bf16),
        ((KINDS * block, bands), bf16),
        ((KINDS * block, bands), bf16),
        ((bands, KINDS * rows), bf16),
        ((twice, width), bf16),
        ((twice, width), bf16),
    ]
    tables = pl.pallas_call(
        filter_kernel,
        in_specs=[SMEM, VMEM, VMEM, VMEM],
        out_specs=[VMEM] * len(shapes),
        out_shape=[jax.ShapeDtypeStruct(shape, kind) for shape, kind in shapes],
        scratch_shapes=[
            pltpu.VMEM((3 * width, width), bf16),
            pltpu.VMEM((3 * rows, KINDS * rows), bf16),
            pltpu.VMEM((3 * rows, KINDS * block), bf16),
            pltpu.VMEM((3 * rows, KINDS * block), bf16),
            pltpu.VMEM((KINDS * rows, 3 * rows), bf16),
        ],
        compiler_params=params(40),
        cost_estimate=pl.CostEstimate(
            flops=4_000_000_000, bytes_accessed=8 << 20, transcendentals=1 << 20
        ),
    )(sc, info, panel, other)

    scale = 1.0 / (4 * local_count * groups * WINDOW)
    share = bands // groups
    parts = pl.pallas_call(
        partial(contract_kernel, [both for _, both in routes], partner_ids.shape[1], scale, owners),
        in_specs=[VMEM] * (1 + len(routes) + len(shapes)),
        out_specs=VMEM,
        out_shape=jax.ShapeDtypeStruct((groups * owners, 1, block), f32),
        scratch_shapes=[
            pltpu.VMEM((KINDS * rows, bands), f32),
            pltpu.VMEM((twice, twice), f32),
        ],
        compiler_params=params(30),
    )(info, *packs, *tables)

    met = lax.all_to_all(parts, ("bl", "bp"), 0, 0, tiled=True)
    return pl.pallas_call(
        partial(gather_kernel, owners),
        in_specs=[VMEM],
        out_specs=VMEM,
        out_shape=jax.ShapeDtypeStruct((2, bands // owners, share), f32),
        compiler_params=params(8),
    )(met)


def solution(mesh):
    placed = (P("bl", "bp", None), P("bl", None), P("bl", None), P())
    return jax.shard_map(
        body, mesh=mesh, in_specs=placed, out_specs=P(None, "bp", "bl"), check_vma=False
    )
```

time: 47.5 us -> 38.2 us (0.80)
  Pallas kernels: 18.9 us -> 10.5 us
  waiting for transfers between devices: 3.27 us -> 6.22 us
  blocking collectives: 13.3 us -> 11 us
  other arithmetic: 0.87 us -> 0.08 us
  local copies, waits for them, and re-layouts: 4.65 us -> 3.92 us
    pallas_call x1, Pallas kernels: 13.1 us -> 6.01 us  [body(): pl.pallas_call(filter_kernel, in_specs=[SMEM, VMEM, VMEM, VMEM], out_spec...]
    ppermute x4, waiting for transfers between devices: 0.01 us -> 2.96 us  [body(): packs = [lax.ppermute(pack, 'bl', route) for route, _ in routes]]
    all_to_all x1, blocking collectives: 13.3 us -> 11 us  [body(): met = lax.all_to_all(parts, ('bl', 'bp'), 0, 0, tiled=True)]
    pallas_call x3, Pallas kernels: 5.75 us -> 4.52 us  [the longest x1 2.96 us: body(): pl.pallas_call(partial(contract_kernel, [both for _, both in routes], par...]
    all_to_all x1 -> x0, other arithmetic: 0.8 us -> none  [body(): met = lax.all_to_all(parts, ('bl', 'bp'), 0, 0, tiled=True)]
    all_to_all x1 -> x0, local copies, waits for them, and re-layouts: 0.51 us -> none  [body(): met = lax.all_to_all(parts, ('bl', 'bp'), 0, 0, tiled=True)]
    unnamed x12 -> x8, local copies, waits for them, and re-layouts: 3.47 us -> 3.25 us
  transfers between devices with their start and end apart: 5 -> 5, of which waited for: 1 -> 3; matrix products, arithmetic and copies ran while one was open for 0% -> 0% of each run, Pallas kernels for 28% -> 16%
where the time goes in v2:
time: 38.2 us; the launch traced here: 38 us
  blocking collectives  11 us (29%)
  Pallas kernels  10.5 us (27%)
  waiting for transfers between devices  6.22 us (16%)
  starting transfers between devices  6.16 us (16%)
  local copies, waits for them, and re-layouts  3.92 us (10%)
    all_to_all x1, blocking collectives, body(): met = lax.all_to_all(parts, ('bl', 'bp'), 0, 0, tiled=True)  11 us
    pallas_call x1, Pallas kernels, body(): pl.pallas_call(filter_kernel, in_specs=[SMEM, VMEM, VMEM, VMEM], out_spec...  6.01 us
    ppermute x1, waiting for transfers between devices, body(): lax.ppermute(diag, 'bp', [(place, place ^ 1) for place in range(owners)])  3.26 us
    unnamed x8, local copies, waits for them, and re-layouts  3.25 us
    ppermute x1, starting transfers between devices, body(): lax.ppermute(diag, 'bp', [(place, place ^ 1) for place in range(owners)])  3.12 us
    ppermute x4, starting transfers between devices, body(): packs = [lax.ppermute(pack, 'bl', route) for route, _ in routes]  3.04 us
    ppermute x4, waiting for transfers between devices, body(): packs = [lax.ppermute(pack, 'bl', route) for route, _ in routes]  2.96 us
    pallas_call x1, Pallas kernels, body(): pl.pallas_call(partial(contract_kernel, [both for _, both in routes], par...  2.96 us
  transfers between devices with their start and end apart: 5, of which 3 were waited for; matrix products, arithmetic and copies ran while one was open for 0% of the time, Pallas kernels for 16%

profile of v2, /device:TPU:0, one launch (start us, length us, event | category | flops | bytes accessed | tf_op | source)
XLA Modules:
  0.0 38.0 jit_solution(17070911095110892451)
XLA Ops:
  0.0 0.1 pad_add_fusion.sc
  0.1 0.0 copy-start
  0.1 1.2 %copy-done = f32[1,256,1024]{2,1,0:T(8,128)S(1)} copy-done((f32[1,256,1024]{2,1,0:T(8,128)S(1)}, f32[1,256,1024]{2,1,0:T(8,128)}, u32[]{:S(2)}) %copy-start) | copy-done | bytes 1048600
  1.3 0.0 copy-start.1
  1.3 0.7 %copy-done.1 = s32[1,1024]{1,0:T(1,128)S(1)} copy-done((s32[1,1024]{1,0:T(1,128)S(1)}, s32[1,1024]{1,0:T(1,128)}, u32[]{:S(2)}) %copy-start.1) | copy-done | bytes 4120
  2.0 0.0 copy-start.2
  2.0 0.7 %copy-done.2 = s32[2,64]{1,0:T(2,128)S(1)} copy-done((s32[2,64]{1,0:T(2,128)S(1)}, s32[2,64]{1,0:T(2,128)}, u32[]{:S(2)}) %copy-start.2) | copy-done | bytes 536
  2.7 0.0 copy-start.3
  2.7 0.7 %copy-done.3 = s32[1,2]{1,0:T(1,128)S(1)} copy-done((s32[1,2]{1,0:T(1,128)S(1)}, s32[1,2]{1,0:T(1,128)}, u32[]{:S(2)}) %copy-start.3) | copy-done | bytes 32
  3.3 1.4 %shard_map.46 = (f32[256,512]{1,0:T(8,128)S(1)}, f32[256,256]{1,0:T(8,128)S(1)}, f32[520,128]{1,0:T(8,128)S(1)}, f32[8,128]{1,0:T(8,128)S(1)}) custom-call(s32[4]{0:T(128)S(1)} %pad_add_fusion.sc, f32[1,256,1024]{2,1,0:T(8,128)S(1)} %copy-done, s32[1,1024]{1,0:T(1,128)S(1)} %copy-done.1, s32[1,2]{1,0:T(1,128)S(1)} %copy-done.3, s32[2,64]{1,0:T(2,128)S(1)} %copy-done.2), custom_call_target="tpu_custom_call" | custom-call | tf_op jit(solution)/shard_map/pallas_call | solution.py:444
  4.7 3.1 %collective-permute-start.4 = (f32[256,256]{1,0:T(8,128)S(1)}, f32[256,256]{1,0:T(8,128)S(1)}, u32[]{:S(2)}, u32[]{:S(2)}) collective-permute-start(f32[256,256]{1,0:T(8,128)S(1)} %get-tuple-element.24), channel_id=1, source_target_pairs={{0,1},{1,0},{2,3},{3,2},{4,5},{5,4},{6,7},{7,6},{8,9},{9,8},{10,11... | collective-permute-start | bytes 786440 | tf_op jit(solution)/shard_map/ppermute | solution.py:464
  7.9 2.4 %collective-permute-start = (f32[520,128]{1,0:T(8,128)S(1)}, f32[520,128]{1,0:T(8,128)S(1)}, u32[]{:S(2)}, u32[]{:S(2)}) collective-permute-start(f32[520,128]{1,0:T(8,128)S(1)} %get-tuple-element.22), channel_id=1, source_target_pairs={{0,24},{4,28},{8,16},{12,20},{16,12},{20,8},{24,4},{28,0},{1,25},{... | collective-permute-start | bytes 798728 | tf_op jit(solution)/shard_map/ppermute | solution.py:466
  10.3 0.5 %collective-permute-start.1 = (f32[520,128]{1,0:T(8,128)S(1)}, f32[520,128]{1,0:T(8,128)S(1)}, u32[]{:S(2)}, u32[]{:S(2)}) collective-permute-start(f32[520,128]{1,0:T(8,128)S(1)} %get-tuple-element.22), channel_id=1, source_target_pairs={{0,8},{4,12},{8,4},{12,0},{16,24},{20,28},{24,20},{28,16},{1,9},{5... | collective-permute-start | bytes 798728 | tf_op jit(solution)/shard_map/ppermute | solution.py:466
  10.8 0.0 collective-permute-start.2
  10.9 0.0 collective-permute-start.3
  10.9 3.3 %collective-permute-done.4.other = f32[256,256]{1,0:T(8,128)S(1)} collective-permute-done((f32[256,256]{1,0:T(8,128)S(1)}, f32[256,256]{1,0:T(8,128)S(1)}, u32[]{:S(2)}, u32[]{:S(2)}) %collective-permute-start.4) | collective-permute-done | bytes 262176 | tf_op jit(solution)/shard_map/ppermute | solution.py:464
  14.2 6.0 %shard_map.47 = (f32[2560,256]{1,0:T(8,128)S(1)}, f32[1024,512]{1,0:T(8,128)S(1)}, f32[128,1024]{1,0:T(8,128)S(1)}, f32[128,512]{1,0:T(8,128)S(1)}, f32[128,512]...) custom-call(s32[4]{0:T(128)S(1)} %pad_add_fusion.sc, ...), custom_call_target="tpu_custom_call" | custom-call | flops 4000000000 | bytes 8388608 | tf_op jit(solution)/shard_map/pallas_call | solution.py:483
  20.2 0.0 collective-permute-done.refs_0_
  20.2 1.2 %collective-permute-done.1.refs_1_ = f32[520,128]{1,0:T(8,128)S(1)} collective-permute-done((f32[520,128]{1,0:T(8,128)S(1)}, f32[520,128]{1,0:T(8,128)S(1)}, u32[]{:S(2)}, u32[]{:S(2)}) %collective-permute-start.1) | collective-permute-done | bytes 266272 | tf_op jit(solution)/shard_map/ppermute | solution.py:466
  21.4 1.7 %collective-permute-done.2.refs_2_ = f32[520,128]{1,0:T(8,128)S(1)} collective-permute-done((f32[520,128]{1,0:T(8,128)S(1)}, f32[520,128]{1,0:T(8,128)S(1)}, u32[]{:S(2)}, u32[]{:S(2)}) %collective-permute-start.2) | collective-permute-done | bytes 266272 | tf_op jit(solution)/shard_map/ppermute | solution.py:466
  23.2 0.0 collective-permute-done.3.refs_3_
  23.2 3.0 %shard_map.48 = f32[32,1,128]{2,1,0:T(1,128)S(1)} custom-call(f32[8,128]{1,0:T(8,128)S(1)} %get-tuple-element.21.info, f32[520,128]{1,0:T(8,128)S(1)} %collective-permute-done.refs_0_, f32[520,128]{1,0:T(8,128)S(1)} %collective-permute-done.1.refs_1_, f32[520,128]{1,0:T(8,128)S(1)} %collective-permute-done.2.refs_2_, ...), custom_call_target="tpu_custom_call" | custom-call | tf_op jit(solution)/shard_map/pallas_call | solution.py:503
  26.1 11.0 %all_to_all.5.parts = f32[32,1,128]{2,1,0:T(1,128)S(1)} all-to-all(f32[32,1,128]{2,1,0:T(1,128)S(1)} %shard_map.48), channel_id=1, replica_groups=mesh['bl'=8,'bp'=4] {'bl','bp'}, dimensions={0} | all-to-all | bytes 32768 | tf_op jit(solution)/shard_map/all_to_all | solution.py:515
  37.1 0.2 shard_map.49
  37.3 0.7 %copy.5 = f32[2,16,8]{1,2,0:T(8,128)} copy(f32[2,16,8]{2,1,0:T(8,128)S(1)} %shard_map.49) | data formatting | bytes 2048 | tf_op jit(solution)/shard_map/pallas_call | solution.py:516
Async XLA Ops:
  0.1 1.2 %copy-start = (f32[1,256,1024]{2,1,0:T(8,128)S(1)}, f32[1,256,1024]{2,1,0:T(8,128)}, u32[]{:S(2)}) copy-start(f32[1,256,1024]{2,1,0:T(8,128)} %cov_hbm.1) | copy-start | bytes 3145732
  1.3 0.7 %copy-start.1 = (s32[1,1024]{1,0:T(1,128)S(1)}, s32[1,1024]{1,0:T(1,128)}, u32[]{:S(2)}) copy-start(s32[1,1024]{1,0:T(1,128)} %keep_hbm.1) | copy-start | bytes 12292
  2.0 0.7 %copy-start.2 = (s32[2,64]{1,0:T(2,128)S(1)}, s32[2,64]{1,0:T(2,128)}, u32[]{:S(2)}) copy-start(s32[2,64]{1,0:T(2,128)} %starts_hbm.1) | copy-start | bytes 1540
  2.7 0.7 %copy-start.3 = (s32[1,2]{1,0:T(1,128)S(1)}, s32[1,2]{1,0:T(1,128)}, u32[]{:S(2)}) copy-start(s32[1,2]{1,0:T(1,128)} %pid_hbm.1) | copy-start | bytes 28
  4.7 9.4 %collective-permute-start.4 = (f32[256,256]{1,0:T(8,128)S(1)}, f32[256,256]{1,0:T(8,128)S(1)}, u32[]{:S(2)}, u32[]{:S(2)}) collective-permute-start(f32[256,256]{1,0:T(8,128)S(1)} %get-tuple-element.24), channel_id=1, source_target_pairs={{0,1},{1,0},{2,3},{3,2},{4,5},{5,4},{6,7},{7,6},{8,9},{9,8},{10,11... | collective-permute-start | bytes 786440 | tf_op jit(solution)/shard_map/ppermute | solution.py:464
  7.9 12.3 %collective-permute-start = (f32[520,128]{1,0:T(8,128)S(1)}, f32[520,128]{1,0:T(8,128)S(1)}, u32[]{:S(2)}, u32[]{:S(2)}) collective-permute-start(f32[520,128]{1,0:T(8,128)S(1)} %get-tuple-element.22), channel_id=1, source_target_pairs={{0,24},{4,28},{8,16},{12,20},{16,12},{20,8},{24,4},{28,0},{1,25},{... | collective-permute-start | bytes 798728 | tf_op jit(solution)/shard_map/ppermute | solution.py:466
  10.3 11.1 %collective-permute-start.1 = (f32[520,128]{1,0:T(8,128)S(1)}, f32[520,128]{1,0:T(8,128)S(1)}, u32[]{:S(2)}, u32[]{:S(2)}) collective-permute-start(f32[520,128]{1,0:T(8,128)S(1)} %get-tuple-element.22), channel_id=1, source_target_pairs={{0,8},{4,12},{8,4},{12,0},{16,24},{20,28},{24,20},{28,16},{1,9},{5... | collective-permute-start | bytes 798728 | tf_op jit(solution)/shard_map/ppermute | solution.py:466
  10.8 12.3 %collective-permute-start.2 = (f32[520,128]{1,0:T(8,128)S(1)}, f32[520,128]{1,0:T(8,128)S(1)}, u32[]{:S(2)}, u32[]{:S(2)}) collective-permute-start(f32[520,128]{1,0:T(8,128)S(1)} %get-tuple-element.22), channel_id=1, source_target_pairs={{0,16},{4,20},{8,24},{12,28},{16,4},{20,0},{24,12},{28,8},{1,17},{... | collective-permute-start | bytes 798728 | tf_op jit(solution)/shard_map/ppermute | solution.py:466
  10.9 12.3 %collective-permute-start.3 = (f32[520,128]{1,0:T(8,128)S(1)}, f32[520,128]{1,0:T(8,128)S(1)}, u32[]{:S(2)}, u32[]{:S(2)}) collective-permute-start(f32[520,128]{1,0:T(8,128)S(1)} %get-tuple-element.22), channel_id=1, source_target_pairs={{0,4},{4,0},{8,12},{12,8},{16,20},{20,16},{24,28},{28,24},{1,5},{5... | collective-permute-start | bytes 798728 | tf_op jit(solution)/shard_map/ppermute | solution.py:466

commit v3 on v2

--- a/solution.py
+++ b/solution.py
@@ -50,7 +50,7 @@
 
 
 def pack_kernel(
-    sc, cov_hbm, keep_hbm, pid_hbm, starts_hbm, panel_out, diag_out, pack_out, info_out,
+    sc, cov_hbm, keep_hbm, pid_hbm, starts_hbm, panel_out, diag_out, info_out, pack_out,
     cov, keep, pid, starts, sems,
 ):
     rows, width = cov.shape
@@ -86,10 +86,6 @@
     diag_out[block:, block:] = jnp.where(first, d00, d11)
     above = iota((block, block), 0) < iota((block, block), 1)
     on = iota((block, block), 0) == iota((block, block), 1)
-    pack_out[:block] = d01
-    pack_out[block : 2 * block] = jnp.where(above, d00, d11)
-    pack_out[2 * block : 3 * block] = c0[:block]
-    pack_out[3 * block : 4 * block] = c1[block:]
     line = iota((8, block), 0)
     info = jnp.where(line == 0, jnp.sum(jnp.where(on, d00, 0.0), axis=0, keepdims=True), 0.0)
     info = jnp.where(line == 1, sc[3].astype(f32), info)
@@ -97,8 +93,10 @@
         info = jnp.where(line == 2 + slot, pid[0, slot].astype(f32), info)
     begin = jnp.where(sc[0] == 0, starts[0:1, :], starts[1:2, :]).astype(f32)
     info = jnp.where(line == 7, jnp.concatenate([begin, begin], axis=1), info)
+    info_out[...] = info
+    for at, value in enumerate((d01, jnp.where(above, d00, d11), c0[:block], c1[block:])):
+        pack_out[at * block : (at + 1) * block] = value
     pack_out[4 * block :] = info
-    info_out[...] = info
 
 
 def turn(x):
@@ -113,30 +111,53 @@
     return (offset >= 0) & (offset < WINDOW)
 
 
-def filter_kernel(
-    sc, info, panel, other,
-    td_out, to_out, hd_out, h0_out, h1_out, q_out,
+def edge_tools(sc, rows, block):
+    first = sc[1] == 0
+
+    def own_place(index):
+        return index + jnp.where(first, 0, rows)
+
+    def other_place(index):
+        return jnp.where(first, index + rows, (index + block) % rows)
+
+    def fade(place, shape, dim):
+        return jnp.exp(jnp.abs(place.astype(f32) - (rows - 0.5)) * decay(shape, dim))
+
+    return own_place, other_place, fade
+
+
+def outside(offset, bands):
+    shape = offset.shape
+    reach = jnp.where(iota(shape, 0) >= bands, offset - WINDOW, -1.0 - offset)
+    return jnp.where(
+        reach >= 0, jnp.exp(jnp.where(reach >= 0, reach, 0.0) * decay(shape, 0)), 0.0
+    )
+
+
+def inside(offset, bands):
+    shape = offset.shape
+    reach = jnp.where(iota(shape, 0) >= bands, WINDOW - offset, offset + 1.0)
+    return jnp.where(
+        held(offset), jnp.exp(jnp.where(held(offset), reach, 0.0) * decay(shape, 0)), 0.0
+    )
+
+
+def prepare_kernel(
+    sc, info, panel,
+    td_out, to_out, hd_out, er_out, ec_out, eo_out, q_out, kc0, kc1,
     bd_out, b0_out, b1_out, br_out, rh_out, rl_out,
-    p3, kr, kc0, kc1, kl,
+    p3, kr, kl,
 ):
     first = sc[1] == 0
     rows, width = panel.shape
     block = rows // 2
     twice = info.shape[1]
     bands = twice // 2
+    own_place, other_place, fade = edge_tools(sc, rows, block)
 
     high, low = split(panel[...])
-    p3[0:rows, :] = high
-    p3[rows : 2 * rows, :] = high
-    p3[2 * rows : 3 * rows, :] = low
-    high, low = split(turn(panel[:, rows:]))
-    p3[3 * rows : 4 * rows, :rows] = high
-    p3[4 * rows : 5 * rows, :rows] = high
-    p3[5 * rows :, :rows] = low
-    high, low = split(other[...])
-    p3[3 * rows : 4 * rows, rows:] = high
-    p3[4 * rows : 5 * rows, rows:] = high
-    p3[5 * rows :, rows:] = low
+    for third, part in enumerate((high, high, low)):
+        p3[third * rows : (third + 1) * rows, :] = part
 
     for chunk in range(2):
         shape = (block, rows)
@@ -160,77 +181,54 @@
                 kc0[third * rows + here : third * rows + here + block, at] = part[:, :block]
                 kc1[third * rows + here : third * rows + here + block, at] = part[:, block:]
 
-    def own_place(index):
-        return index + jnp.where(first, 0, rows)
-
-    def other_place(index):
-        return jnp.where(first, index + rows, (index + block) % rows)
-
-    def gap(place):
-        return jnp.abs(place.astype(f32) - (rows - 0.5))
-
     shape = (rows, twice)
-    own_column = jnp.exp(gap(own_place(iota(shape, 0))) * decay(shape, 1))
-    other_column = jnp.exp(gap(other_place(iota(shape, 0))) * decay(shape, 1))
+    own_column = fade(own_place(iota(shape, 0)), shape, 1)
+    other_column = fade(other_place(iota(shape, 0)), shape, 1)
     shape = (8, rows)
-    own_row = jnp.exp(gap(own_place(iota(shape, 1))) * decay(shape, 0))
-    other_row = jnp.exp(gap(other_place(iota(shape, 1))) * decay(shape, 0))
+    own_row = fade(own_place(iota(shape, 1)), shape, 0)
+    other_row = fade(other_place(iota(shape, 1)), shape, 0)
 
     begin = info[7:8, :]
     begin_column = turn(jnp.broadcast_to(begin, (twice, twice)))[:, :1]
-
-    extra = 16
     shape = (twice, rows)
-    after = iota(shape, 0) >= bands
-
-    def outside(place):
-        offset = place.astype(f32) - begin_column
-        reach = jnp.where(after, offset - WINDOW, -1.0 - offset)
-        return jnp.where(
-            reach >= 0, jnp.exp(jnp.where(reach >= 0, reach, 0.0) * decay(shape, 0)), 0.0
-        )
-
-    def inside(place):
-        offset = place.astype(f32) - begin_column
-        reach = jnp.where(after, WINDOW - offset, offset + 1.0)
-        return jnp.where(
-            held(offset), jnp.exp(jnp.where(held(offset), reach, 0.0) * decay(shape, 0)), 0.0
-        )
-
+    own_offset = own_place(iota(shape, 1)).astype(f32) - begin_column
+    other_offset = other_place(iota(shape, 1)).astype(f32) - begin_column
     none = jnp.zeros((8, rows), f32)
     four = iota((8, rows), 0) < KINDS
-    out_own = outside(own_place(iota(shape, 1)))
-    out_other = outside(other_place(iota(shape, 1)))
-    weights_own = jnp.concatenate([out_own, jnp.where(four, 0.0, own_row), none], axis=0)
-    weights_other = jnp.concatenate([out_other, jnp.where(four, other_row, 0.0), none], axis=0)
-    lhs = jnp.concatenate([left3(weights_own), left3(weights_other)], axis=1)
-    edge = dot(lhs, p3[...])
-    edge_own = left3(edge[:, :rows])
-    edge_other = left3(edge[:, rows:])
-    from_other = dot(edge_other, right3(other_column))
-    from_own = dot(edge_own, right3(own_column))
-    near = jnp.concatenate([left3(edge[:twice, :rows]), left3(edge[:twice, rows:])], axis=1)
-    flip_own, flip_own_low = split(out_own)
-    flip_other, flip_other_low = split(out_other)
-    q_out[...] = dot_t(
-        near,
-        jnp.concatenate(
-            [flip_own, flip_own, flip_own_low, flip_other, flip_other, flip_other_low], axis=1
-        ),
-    )
+    weights_own = jnp.concatenate(
+        [outside(own_offset, bands), jnp.where(four, 0.0, own_row), none], axis=0
+    )
+    weights_other = jnp.concatenate(
+        [outside(other_offset, bands), jnp.where(four, other_row, 0.0), none], axis=0
+    )
+    part = dot(left3(weights_own), p3[...])
+    edge_c = part[:, rows:]
+    edge_r = part[:, :rows] + dot(left3(weights_other), right3(turn(panel[:, rows:])))
+    left_r = left3(edge_r)
+    from_own = dot(left_r, right3(own_column))
+    from_other = dot(left3(edge_c), right3(other_column))
+    er_out[...] = from_own
+    ec_out[...] = edge_c
+    eo_out[...] = weights_other
+    high, low = split(weights_own)
+    q_out[...] = dot_t(left_r, jnp.concatenate([high, high, low], axis=1)[:twice])[:twice]
     for kind in range(KINDS):
         at = slice(kind * rows, (kind + 1) * rows)
-        full = dot(edge_own, kr[:, at]) + from_other[:, kind : kind + 1] * own_row[kind : kind + 1]
-        hd_out[:, at] = full[:twice]
-        turned = turn(full[twice : twice + 8])
-        value = dot(kl[at, :], p3[: 3 * rows, :])
-        value = value + own_column[:, kind : kind + 1] * edge[twice + kind : twice + kind + 1, :]
-        left_own = left3(value[:, :rows])
+        full = dot(left_r, kr[:, at])
+        hd_out[:, at] = full
+        near = full[twice : twice + 8]
+        near = near + jnp.where(
+            four, 0.0, from_other[twice : twice + 8, kind : kind + 1] * own_row[kind : kind + 1]
+        )
+        turned = turn(near)
+        value = dot(kl[at, :], p3[...])
+        carry = edge_r[twice + kind : twice + kind + 1, :]
+        left_own = left3(value[:, :rows] + own_column[:, kind : kind + 1] * carry)
         left_other = left3(value[:, rows:])
         for second in range(kind, KINDS):
             here = slice(second * rows, (second + 1) * rows)
-            to = pair_index(kind, second) * rows
-            td_out[to : to + rows, :] = (
+            spot = pair_index(kind, second) * rows
+            td_out[spot : spot + rows, :] = (
                 dot(left_own, kr[:, here])
                 + turned[:, second : second + 1] * own_row[second : second + 1]
             )
@@ -246,14 +244,6 @@
             to_out[kind * rows + block : (kind + 1) * rows, here] = (
                 bottom[:, here] + column[block:] * line[:, block:]
             )
-    high0 = dot(edge_other[:twice], kc0[...])
-    high1 = dot(edge_other[:twice], kc1[...])
-    for kind in range(KINDS):
-        here = slice(kind * block, (kind + 1) * block)
-        column = from_own[:twice, kind : kind + 1]
-        line = other_row[kind : kind + 1]
-        h0_out[:, here] = high0[:, here] + column * line[:, :block]
-        h1_out[:, here] = high1[:, here] + column * line[:, block:]
 
     begins = begin[:, :bands]
 
@@ -267,17 +257,64 @@
     bd_out[...] = boxes(rows, own_place)
     b0_out[...] = boxes(block, other_place)
     b1_out[...] = boxes(block, lambda index: other_place(index + block))
-    shape2 = (bands, KINDS * rows)
-    index = iota(shape2, 1)
+    shape = (bands, KINDS * rows)
+    index = iota(shape, 1)
     hit = held(own_place(index % rows).astype(f32) - begin_column[:bands])
-    hit = hit & (iota(shape2, 0) % KINDS == index // rows)
+    hit = hit & (iota(shape, 0) % KINDS == index // rows)
     br_out[...] = jnp.where(hit, 1.0, 0.0).astype(bf16)
-    high, low = split(inside(own_place(iota(shape, 1))))
+    high, low = split(inside(own_offset, bands))
     rh_out[:, :rows] = high
     rl_out[:, :rows] = low
-    high, low = split(inside(other_place(iota(shape, 1))))
+    high, low = split(inside(other_offset, bands))
     rh_out[:, rows:] = high
     rl_out[:, rows:] = low
+
+
+def finish_kernel(
+    sc, other, td, to, hd, er, ec, eo, q, kc0, kc1,
+    td_out, to_out, hd_out, h0_out, h1_out, q_out,
+):
+    rows = other.shape[0]
+    block = rows // 2
+    twice = q.shape[0]
+    own_place, other_place, fade = edge_tools(sc, rows, block)
+    shape = (rows, twice)
+    own_column = fade(own_place(iota(shape, 0)), shape, 1)
+    other_column = fade(other_place(iota(shape, 0)), shape, 1)
+    shape = (8, rows)
+    own_row = fade(own_place(iota(shape, 1)), shape, 0)
+    other_row = fade(other_place(iota(shape, 1)), shape, 0)
+    edge_c = ec[...] + dot(left3(eo[...]), right3(other[...]))
+    left_c = left3(edge_c)
+    high, low = split(eo[...])
+    q_out[...] = (
+        q[...] + dot_t(left_c, jnp.concatenate([high, high, low], axis=1)[:twice])[:twice]
+    )
+    from_other = dot(left_c, right3(other_column))
+    high0 = dot(left_c, kc0[...])
+    high1 = dot(left_c, kc1[...])
+    for kind in range(KINDS):
+        at = slice(kind * rows, (kind + 1) * rows)
+        hd_out[:, at] = (
+            hd[:twice, at] + from_other[:twice, kind : kind + 1] * own_row[kind : kind + 1]
+        )
+        here = slice(kind * block, (kind + 1) * block)
+        column = er[:twice, kind : kind + 1]
+        line = other_row[kind : kind + 1]
+        h0_out[:, here] = high0[:twice, here] + column * line[:, :block]
+        h1_out[:, here] = high1[:twice, here] + column * line[:, block:]
+        column = own_column[:, kind : kind + 1]
+        for second in range(kind, KINDS):
+            spot = pair_index(kind, second) * rows
+            line = own_row[second : second + 1] * from_other[
+                twice + second : twice + second + 1, kind : kind + 1
+            ]
+            td_out[spot : spot + rows, :] = td[spot : spot + rows, :] + column * line
+        mid = kind * rows + block
+        end = (kind + 1) * rows
+        line = slice(twice + kind, twice + kind + 1)
+        to_out[kind * rows : mid, :] = to[kind * rows : mid, :] + column[:block] * high0[line, :]
+        to_out[mid:end, :] = to[mid:end, :] + column[block:] * high1[line, :]
 
 
 def pair_index(kind, second):
@@ -293,7 +330,7 @@
     bands = bd.shape[1]
     twice = 2 * bands
     own = info[...]
-    total = extra = None
+    total = extra = 0.0
     for pack, both in zip(packs, peer_counts):
         aux = pack[4 * block :, :]
         weight = jnp.zeros_like(aux[:1])
@@ -302,10 +339,8 @@
             weight = weight + jnp.where(aux[1:2] == own[at], 1.0, 0.0)
             if both:
                 weight = weight + jnp.where(aux[at] == own[1:2], 1.0, 0.0)
-        part = pack[: 4 * block, :] * weight
-        line = aux[0:1, :] * weight
-        total = part if total is None else total + part
-        extra = line if extra is None else extra + line
+        total = total + pack[: 4 * block, :] * weight
+        extra = extra + aux[0:1, :] * weight
     upper = total[:block]
     tri = total[block : 2 * block]
     flipped = turn(tri)
@@ -395,7 +430,7 @@
 
 def gather_kernel(owners, parts, out):
     per_half = owners // 2
-    lines, share = out.shape[1], out.shape[2]
+    share, lines = out.shape[1], out.shape[2]
     lanes = parts.shape[2]
     for half in range(2):
         acc = None
@@ -403,12 +438,9 @@
             for place in range(per_half):
                 value = parts[first + half * per_half + place]
                 acc = value if acc is None else acc + value
-        line = iota((lanes, lanes), 0)
-        table = jnp.zeros((lanes, lanes), f32)
         for member in range(share):
             value = pltpu.roll(acc, (-member * lines) % lanes, 1) if member else acc
-            table = jnp.where(line == member, value, table)
-        out[half] = turn(table)[:lines, :share]
+            out[half, member : member + 1, :] = value[:, :lines]
 
 
 def partner_routes(groups):
@@ -428,6 +460,10 @@
         ([(source, (source - hop) % groups) for source in range(groups)], False)
         for hop in range(1, GROUP_REACH + 1)
     ]
+
+
+def in_hbm(value):
+    return pltpu.with_memory_space_constraint(value, pltpu.HBM)
 
 
 def body(inverse_cov, channel_keep_mask, partner_ids, band_starts):
@@ -441,15 +477,15 @@
     assert local_count == 1 and width == 2 * rows and block == 128 == twice
     owner, group = lax.axis_index("bp"), lax.axis_index("bl")
     sc = jnp.stack([owner // per_half, owner % per_half, owner, group]).astype(jnp.int32)
-    panel, diag, pack, info = pl.pallas_call(
+    panel, diag, info, pack = pl.pallas_call(
         pack_kernel,
         in_specs=[SMEM, HBM, HBM, HBM, HBM],
         out_specs=[VMEM] * 4,
         out_shape=[
             jax.ShapeDtypeStruct((rows, width), f32),
             jax.ShapeDtypeStruct((rows, rows), f32),
+            jax.ShapeDtypeStruct((8, block), f32),
             jax.ShapeDtypeStruct((4 * block + 8, block), f32),
-            jax.ShapeDtypeStruct((8, block), f32),
         ],
         scratch_shapes=[
             pltpu.VMEM((rows, width), f32),
@@ -459,20 +495,30 @@
             pltpu.SemaphoreType.DMA((4,)),
         ],
         compiler_params=params(16),
-    )(sc, inverse_cov, channel_keep_mask, partner_ids, band_starts)
+    )(
+        sc,
+        in_hbm(inverse_cov),
+        in_hbm(channel_keep_mask),
+        in_hbm(partner_ids),
+        in_hbm(band_starts),
+    )
 
     other = lax.ppermute(diag, "bp", [(place, place ^ 1) for place in range(owners)])
     routes = partner_routes(groups)
-    packs = [lax.ppermute(pack, "bl", route) for route, _ in routes]
+    arrived = [lax.ppermute(pack, "bl", route) for route, _ in routes]
 
     pairs = KINDS * (KINDS + 1) // 2
+    lines = twice + 16
     shapes = [
         ((pairs * rows, rows), f32),
         ((KINDS * rows, KINDS * block), f32),
-        ((twice, KINDS * rows), f32),
-        ((twice, KINDS * block), f32),
-        ((twice, KINDS * block), f32),
+        ((lines, KINDS * rows), f32),
+        ((lines, twice), f32),
+        ((lines, rows), f32),
+        ((lines, rows), f32),
         ((twice, twice), f32),
+        ((3 * rows, KINDS * block), bf16),
+        ((3 * rows, KINDS * block), bf16),
         ((KINDS * rows, bands), bf16),
         ((KINDS * block, bands), bf16),
         ((KINDS * block, bands), bf16),
@@ -480,29 +526,47 @@
         ((twice, width), bf16),
         ((twice, width), bf16),
     ]
-    tables = pl.pallas_call(
-        filter_kernel,
-        in_specs=[SMEM, VMEM, VMEM, VMEM],
+    begun = pl.pallas_call(
+        prepare_kernel,
+        in_specs=[SMEM, VMEM, VMEM],
         out_specs=[VMEM] * len(shapes),
         out_shape=[jax.ShapeDtypeStruct(shape, kind) for shape, kind in shapes],
         scratch_shapes=[
-            pltpu.VMEM((3 * width, width), bf16),
+            pltpu.VMEM((3 * rows, width), bf16),
             pltpu.VMEM((3 * rows, KINDS * rows), bf16),
-            pltpu.VMEM((3 * rows, KINDS * block), bf16),
-            pltpu.VMEM((3 * rows, KINDS * block), bf16),
             pltpu.VMEM((KINDS * rows, 3 * rows), bf16),
         ],
-        compiler_params=params(40),
+        compiler_params=params(36),
         cost_estimate=pl.CostEstimate(
             flops=4_000_000_000, bytes_accessed=8 << 20, transcendentals=1 << 20
         ),
-    )(sc, info, panel, other)
+    )(sc, info, panel)
+    ends = shapes[:2] + [
+        ((twice, KINDS * rows), f32),
+        ((twice, KINDS * block), f32),
+        ((twice, KINDS * block), f32),
+        ((twice, twice), f32),
+    ]
+    tables = pl.pallas_call(
+        finish_kernel,
+        in_specs=[SMEM] + [VMEM] * 10,
+        out_specs=[VMEM] * len(ends),
+        out_shape=[jax.ShapeDtypeStruct(shape, kind) for shape, kind in ends],
+        input_output_aliases={2: 0, 3: 1},
+        compiler_params=params(16),
+        cost_estimate=pl.CostEstimate(
+            flops=2_000_000_000, bytes_accessed=8 << 20, transcendentals=1 << 17
+        ),
+    )(sc, other, *begun[:9])
+    tables = [*tables, *begun[9:]]
 
     scale = 1.0 / (4 * local_count * groups * WINDOW)
     share = bands // groups
     parts = pl.pallas_call(
-        partial(contract_kernel, [both for _, both in routes], partner_ids.shape[1], scale, owners),
-        in_specs=[VMEM] * (1 + len(routes) + len(shapes)),
+        partial(
+            contract_kernel, [both for _, both in routes], partner_ids.shape[1], scale, owners
+        ),
+        in_specs=[VMEM] * (1 + len(arrived) + len(tables)),
         out_specs=VMEM,
         out_shape=jax.ShapeDtypeStruct((groups * owners, 1, block), f32),
         scratch_shapes=[
@@ -510,16 +574,17 @@
             pltpu.VMEM((twice, twice), f32),
         ],
         compiler_params=params(30),
-    )(info, *packs, *tables)
+    )(info, *arrived, *tables)
 
     met = lax.all_to_all(parts, ("bl", "bp"), 0, 0, tiled=True)
-    return pl.pallas_call(
+    turned = pl.pallas_call(
         partial(gather_kernel, owners),
         in_specs=[VMEM],
         out_specs=VMEM,
-        out_shape=jax.ShapeDtypeStruct((2, bands // owners, share), f32),
+        out_shape=jax.ShapeDtypeStruct((2, share, bands // owners), f32),
         compiler_params=params(8),
     )(met)
+    return jnp.swapaxes(turned, 1, 2)
 
 
 def solution(mesh):

time: 38.2 us -> 34.7 us (0.908)
  waiting for transfers between devices: 6.22 us -> 1.85 us
  local copies, waits for them, and re-layouts: 3.92 us -> 0 us
  Pallas kernels: 10.5 us -> 13.4 us
  blocking collectives: 11 us -> 13.1 us
    unnamed x8 -> x0, local copies, waits for them, and re-layouts: 3.25 us -> none
    ppermute x4, waiting for transfers between devices: 2.96 us -> 0.58 us  [body(): arrived = [lax.ppermute(pack, 'bl', route) for route, _ in routes]]
    all_to_all x1, blocking collectives: 11 us -> 13.1 us  [body(): met = lax.all_to_all(parts, ('bl', 'bp'), 0, 0, tiled=True)]
    pallas_call x1 -> x2, Pallas kernels: 6.01 us -> 8.01 us  [the longest x1 5.87 us: body(): pl.pallas_call(prepare_kernel, in_specs=[SMEM, VMEM, VMEM], out_specs=[VM...]
    ppermute x1, waiting for transfers between devices: 3.26 us -> 1.27 us  [body(): lax.ppermute(diag, 'bp', [(place, place ^ 1) for place in range(owners)])]
    ppermute x4, starting transfers between devices: 3.04 us -> 4.61 us  [body(): arrived = [lax.ppermute(pack, 'bl', route) for route, _ in routes]]
    ppermute x1, starting transfers between devices: 3.12 us -> 1.58 us  [body(): lax.ppermute(diag, 'bp', [(place, place ^ 1) for place in range(owners)])]
    pallas_call x1 -> x0, local copies, waits for them, and re-layouts: 0.68 us -> none  [body(): pl.pallas_call(partial(gather_kernel, owners), in_specs=[VMEM], out_specs...]
  transfers between devices with their start and end apart: 5 -> 5, of which waited for: 3 -> 2; matrix products, arithmetic and copies ran while one was open for 0% -> 0% of each run, Pallas kernels for 16% -> 23%
where the time goes in v3:
time: 34.7 us; the launch traced here: 34.6 us
  Pallas kernels  13.4 us (39%)
  blocking collectives  13.1 us (38%)
  starting transfers between devices  6.18 us (18%)
  waiting for transfers between devices  1.85 us (5%)
    all_to_all x1, blocking collectives, body(): met = lax.all_to_all(parts, ('bl', 'bp'), 0, 0, tiled=True)  13.1 us
    pallas_call x1, Pallas kernels, body(): pl.pallas_call(prepare_kernel, in_specs=[SMEM, VMEM, VMEM], out_specs=[VM...  5.87 us
    ppermute x4, starting transfers between devices, body(): arrived = [lax.ppermute(pack, 'bl', route) for route, _ in routes]  4.61 us
    pallas_call x1, Pallas kernels, body(): pl.pallas_call(partial(contract_kernel, [both for _, both in routes], par...  2.8 us
    pallas_call x1, Pallas kernels, body(): pl.pallas_call(finish_kernel, in_specs=[SMEM] + [VMEM] * 10, out_specs=[V...  2.15 us
    pallas_call x1, Pallas kernels, body(): pl.pallas_call(pack_kernel, in_specs=[SMEM, HBM, HBM, HBM, HBM], out_spec...  1.86 us
    ppermute x1, starting transfers between devices, body(): lax.ppermute(diag, 'bp', [(place, place ^ 1) for place in range(owners)])  1.58 us
    ppermute x1, waiting for transfers between devices, body(): lax.ppermute(diag, 'bp', [(place, place ^ 1) for place in range(owners)])  1.27 us
  transfers between devices with their start and end apart: 5, of which 2 were waited for; matrix products, arithmetic and copies ran while one was open for 0% of the time, Pallas kernels for 23%

profile of v3, /device:TPU:0, one launch (start us, length us, event | category | flops | bytes accessed | tf_op | source)
XLA Modules:
  0.0 34.6 jit_solution(9809895374381520695)
XLA Ops:
  0.0 0.1 pad_add_fusion.sc
  0.1 1.9 %shard_map.46 = (f32[256,512]{1,0:T(8,128)S(1)}, f32[256,256]{1,0:T(8,128)S(1)}, f32[8,128]{1,0:T(8,128)S(1)}, f32[520,128]{1,0:T(8,128)S(1)}) custom-call(s32[4]{0:T(128)S(1)} %pad_add_fusion.sc, f32[1,256,1024]{2,1,0:T(8,128)} %cov_hbm.1, s32[1,1024]{1,0:T(1,128)} %keep_hbm.1, s32[1,2]{1,0:T(1,128)} %pid_hbm.1, s32[2,64]{1,0:T(2,128)} %starts_hbm.1), custom_call_target="tpu_custom_call" | custom-call | tf_op jit(solution)/shard_map/pallas_call | solution.py:480
  1.9 4.0 %collective-permute-start = (f32[520,128]{1,0:T(8,128)S(1)}, f32[520,128]{1,0:T(8,128)S(1)}, u32[]{:S(2)}, u32[]{:S(2)}) collective-permute-start(f32[520,128]{1,0:T(8,128)S(1)} %get-tuple-element.31), channel_id=1, source_target_pairs={{0,24},{4,28},{8,16},{12,20},{16,12},{20,8},{24,4},{28,0},{1,25},{... | collective-permute-start | bytes 798728 | tf_op jit(solution)/shard_map/ppermute | solution.py:508
  5.9 0.5 %collective-permute-start.1 = (f32[520,128]{1,0:T(8,128)S(1)}, f32[520,128]{1,0:T(8,128)S(1)}, u32[]{:S(2)}, u32[]{:S(2)}) collective-permute-start(f32[520,128]{1,0:T(8,128)S(1)} %get-tuple-element.31), channel_id=1, source_target_pairs={{0,8},{4,12},{8,4},{12,0},{16,24},{20,28},{24,20},{28,16},{1,9},{5... | collective-permute-start | bytes 798728 | tf_op jit(solution)/shard_map/ppermute | solution.py:508
  6.5 0.1 collective-permute-start.2
  6.6 0.0 collective-permute-start.3
  6.6 1.6 %collective-permute-start.4 = (f32[256,256]{1,0:T(8,128)S(1)}, f32[256,256]{1,0:T(8,128)S(1)}, u32[]{:S(2)}, u32[]{:S(2)}) collective-permute-start(f32[256,256]{1,0:T(8,128)S(1)} %get-tuple-element.32), channel_id=1, source_target_pairs={{0,1},{1,0},{2,3},{3,2},{4,5},{5,4},{6,7},{7,6},{8,9},{9,8},{10,11... | collective-permute-start | bytes 786440 | tf_op jit(solution)/shard_map/ppermute | solution.py:506
  8.1 5.9 %shard_map.47 = (f32[2560,256]{1,0:T(8,128)S(1)}, f32[1024,512]{1,0:T(8,128)S(1)}, f32[144,1024]{1,0:T(8,128)S(1)}, f32[144,128]{1,0:T(8,128)S(1)}, f32[144,256]...) custom-call(s32[4]{0:T(128)S(1)} %pad_add_fusion.sc, ...), custom_call_target="tpu_custom_call" | custom-call | flops 4000000000 | bytes 8388608 | tf_op jit(solution)/shard_map/pallas_call | solution.py:529
  14.0 1.3 %collective-permute-done.4.other = f32[256,256]{1,0:T(8,128)S(1)} collective-permute-done((f32[256,256]{1,0:T(8,128)S(1)}, f32[256,256]{1,0:T(8,128)S(1)}, u32[]{:S(2)}, u32[]{:S(2)}) %collective-permute-start.4) | collective-permute-done | bytes 262176 | tf_op jit(solution)/shard_map/ppermute | solution.py:506
  15.3 2.1 %shard_map.48 = (f32[2560,256]{1,0:T(8,128)S(1)}, f32[1024,512]{1,0:T(8,128)S(1)}, f32[128,1024]{1,0:T(8,128)S(1)}, f32[128,512]{1,0:T(8,128)S(1)}, f32[128,512]{1,0:T(8,128)S(1)}, /*index=5*/f32[128,128]{1,0:T(8,128)S(1)}) custom-call(s32[4]{0:T(128)S(1)} %pad_add_fusion.sc, ...), custom_call_target="tpu_custom_call", output_to_operand_aliasing={{0}: (2, {}), {1}: (3, {})} | custom-call | flops 2000000000 | bytes 8388608 | tf_op jit(solution)/shard_map/pallas_call | solution.py:550
  17.4 0.0 collective-permute-done.refs_0_
  17.4 0.0 collective-permute-done.1.refs_1_
  17.5 0.6 %collective-permute-done.2.refs_2_ = f32[520,128]{1,0:T(8,128)S(1)} collective-permute-done((f32[520,128]{1,0:T(8,128)S(1)}, f32[520,128]{1,0:T(8,128)S(1)}, u32[]{:S(2)}, u32[]{:S(2)}) %collective-permute-start.2) | collective-permute-done | bytes 266272 | tf_op jit(solution)/shard_map/ppermute | solution.py:508
  18.0 0.0 collective-permute-done.3.refs_3_
  18.0 2.8 %shard_map.49 = f32[32,1,128]{2,1,0:T(1,128)S(1)} custom-call(f32[8,128]{1,0:T(8,128)S(1)} %get-tuple-element.30.info, f32[520,128]{1,0:T(8,128)S(1)} %collective-permute-done.refs_0_, f32[520,128]{1,0:T(8,128)S(1)} %collective-permute-done.1.refs_1_, f32[520,128]{1,0:T(8,128)S(1)} %collective-permute-done.2.refs_2_, ...), custom_call_target="tpu_custom_call" | custom-call | tf_op jit(solution)/shard_map/pallas_call | solution.py:565
  20.8 13.1 %all_to_all.5.parts = f32[32,1,128]{2,1,0:T(1,128)S(1)} all-to-all(f32[32,1,128]{2,1,0:T(1,128)S(1)} %shard_map.49), channel_id=1, replica_groups=mesh['bl'=8,'bp'=4] {'bl','bp'}, dimensions={0} | all-to-all | bytes 32768 | tf_op jit(solution)/shard_map/all_to_all | solution.py:579
  33.9 0.7 %shard_map.50 = f32[2,8,16]{2,1,0:T(8,128)} custom-call(f32[32,1,128]{2,1,0:T(1,128)S(1)} %all_to_all.5.parts), custom_call_target="tpu_custom_call" | custom-call | tf_op jit(solution)/shard_map/pallas_call | solution.py:580
Async XLA Ops:
  1.9 15.5 %collective-permute-start = (f32[520,128]{1,0:T(8,128)S(1)}, f32[520,128]{1,0:T(8,128)S(1)}, u32[]{:S(2)}, u32[]{:S(2)}) collective-permute-start(f32[520,128]{1,0:T(8,128)S(1)} %get-tuple-element.31), channel_id=1, source_target_pairs={{0,24},{4,28},{8,16},{12,20},{16,12},{20,8},{24,4},{28,0},{1,25},{... | collective-permute-start | bytes 798728 | tf_op jit(solution)/shard_map/ppermute | solution.py:508
  5.9 11.5 %collective-permute-start.1 = (f32[520,128]{1,0:T(8,128)S(1)}, f32[520,128]{1,0:T(8,128)S(1)}, u32[]{:S(2)}, u32[]{:S(2)}) collective-permute-start(f32[520,128]{1,0:T(8,128)S(1)} %get-tuple-element.31), channel_id=1, source_target_pairs={{0,8},{4,12},{8,4},{12,0},{16,24},{20,28},{24,20},{28,16},{1,9},{5... | collective-permute-start | bytes 798728 | tf_op jit(solution)/shard_map/ppermute | solution.py:508
  6.5 11.6 %collective-permute-start.2 = (f32[520,128]{1,0:T(8,128)S(1)}, f32[520,128]{1,0:T(8,128)S(1)}, u32[]{:S(2)}, u32[]{:S(2)}) collective-permute-start(f32[520,128]{1,0:T(8,128)S(1)} %get-tuple-element.31), channel_id=1, source_target_pairs={{0,16},{4,20},{8,24},{12,28},{16,4},{20,0},{24,12},{28,8},{1,17},{... | collective-permute-start | bytes 798728 | tf_op jit(solution)/shard_map/ppermute | solution.py:508
  6.6 11.5 %collective-permute-start.3 = (f32[520,128]{1,0:T(8,128)S(1)}, f32[520,128]{1,0:T(8,128)S(1)}, u32[]{:S(2)}, u32[]{:S(2)}) collective-permute-start(f32[520,128]{1,0:T(8,128)S(1)} %get-tuple-element.31), channel_id=1, source_target_pairs={{0,4},{4,0},{8,12},{12,8},{16,20},{20,16},{24,28},{28,24},{1,5},{5... | collective-permute-start | bytes 798728 | tf_op jit(solution)/shard_map/ppermute | solution.py:508
  6.6 8.7 %collective-permute-start.4 = (f32[256,256]{1,0:T(8,128)S(1)}, f32[256,256]{1,0:T(8,128)S(1)}, u32[]{:S(2)}, u32[]{:S(2)}) collective-permute-start(f32[256,256]{1,0:T(8,128)S(1)} %get-tuple-element.32), channel_id=1, source_target_pairs={{0,1},{1,0},{2,3},{3,2},{4,5},{5,4},{6,7},{7,6},{8,9},{9,8},{10,11... | collective-permute-start | bytes 786440 | tf_op jit(solution)/shard_map/ppermute | solution.py:506

commit v4 on v3

--- a/solution.py
+++ b/solution.py
@@ -13,9 +13,13 @@
 
 f32 = jnp.float32
 bf16 = jnp.bfloat16
-SMEM = pl.BlockSpec(memory_space=pltpu.SMEM)
 VMEM = pl.BlockSpec(memory_space=pltpu.VMEM)
 HBM = pl.BlockSpec(memory_space=pltpu.HBM)
+
+
+def position():
+    owner, per_half = lax.axis_index("bp"), lax.axis_size("bp") // 2
+    return owner // per_half, owner % per_half, lax.axis_index("bl")
 
 
 def params(mib):
@@ -50,11 +54,12 @@
 
 
 def pack_kernel(
-    sc, cov_hbm, keep_hbm, pid_hbm, starts_hbm, panel_out, diag_out, info_out, pack_out,
+    cov_hbm, keep_hbm, pid_hbm, starts_hbm, panel_out, diag_out, info_out, pack_out,
     cov, keep, pid, starts, sems,
 ):
     rows, width = cov.shape
-    columns = pl.ds(pl.multiple_of(sc[0] * width, width), width)
+    half, place, group = position()
+    columns = pl.ds(pl.multiple_of(half * width, width), width)
     copies = [
         pltpu.make_async_copy(cov_hbm.at[0, :, columns], cov, sems.at[0]),
         pltpu.make_async_copy(keep_hbm, keep, sems.at[1]),
@@ -66,9 +71,9 @@
     for copy in copies:
         copy.wait()
     block = rows // 2
-    first = sc[1] == 0
+    first = place == 0
     marks = keep[...].astype(f32)
-    half_marks = jnp.where(sc[0] == 0, marks[:, :width], marks[:, width:])
+    half_marks = jnp.where(half == 0, marks[:, :width], marks[:, width:])
     row_marks = jnp.where(first, half_marks[:, :rows], half_marks[:, rows:])
     row_col = jnp.transpose(jnp.broadcast_to(row_marks, (128, rows)))[:, :1]
     masked = cov[...] * row_col * half_marks
@@ -88,10 +93,10 @@
     on = iota((block, block), 0) == iota((block, block), 1)
     line = iota((8, block), 0)
     info = jnp.where(line == 0, jnp.sum(jnp.where(on, d00, 0.0), axis=0, keepdims=True), 0.0)
-    info = jnp.where(line == 1, sc[3].astype(f32), info)
+    info = jnp.where(line == 1, group.astype(f32), info)
     for slot in range(pid.shape[1]):
-        info = jnp.where(line == 2 + slot, pid[0, slot].astype(f32), info)
-    begin = jnp.where(sc[0] == 0, starts[0:1, :], starts[1:2, :]).astype(f32)
+        info = jnp.where(line == 2 + slot, pid[:, slot : slot + 1].astype(f32), info)
+    begin = jnp.where(half == 0, starts[0:1, :], starts[1:2, :]).astype(f32)
     info = jnp.where(line == 7, jnp.concatenate([begin, begin], axis=1), info)
     info_out[...] = info
     for at, value in enumerate((d01, jnp.where(above, d00, d11), c0[:block], c1[block:])):
@@ -111,8 +116,7 @@
     return (offset >= 0) & (offset < WINDOW)
 
 
-def edge_tools(sc, rows, block):
-    first = sc[1] == 0
+def edge_tools(first, rows, block):
 
     def own_place(index):
         return index + jnp.where(first, 0, rows)
@@ -143,17 +147,17 @@
 
 
 def prepare_kernel(
-    sc, info, panel,
+    info, panel,
     td_out, to_out, hd_out, er_out, ec_out, eo_out, q_out, kc0, kc1,
-    bd_out, b0_out, b1_out, br_out, rh_out, rl_out,
+    bx_out, br_out, bt_out, bl_out, rh_out, rl_out,
     p3, kr, kl,
 ):
-    first = sc[1] == 0
+    first = position()[1] == 0
     rows, width = panel.shape
     block = rows // 2
     twice = info.shape[1]
     bands = twice // 2
-    own_place, other_place, fade = edge_tools(sc, rows, block)
+    own_place, other_place, fade = edge_tools(first, rows, block)
 
     high, low = split(panel[...])
     for third, part in enumerate((high, high, low)):
@@ -254,14 +258,20 @@
         hit = hit & (iota(shape, 1) % KINDS == index // count)
         return jnp.where(hit, 1.0, 0.0).astype(bf16)
 
-    bd_out[...] = boxes(rows, own_place)
-    b0_out[...] = boxes(block, other_place)
-    b1_out[...] = boxes(block, lambda index: other_place(index + block))
-    shape = (bands, KINDS * rows)
-    index = iota(shape, 1)
-    hit = held(own_place(index % rows).astype(f32) - begin_column[:bands])
-    hit = hit & (iota(shape, 0) % KINDS == index // rows)
-    br_out[...] = jnp.where(hit, 1.0, 0.0).astype(bf16)
+    def row_boxes(count, place):
+        shape = (bands, 2 * KINDS * count)
+        index = iota(shape, 1)
+        hit = held(place(index % count).astype(f32) - begin_column[:bands])
+        hit = hit & (iota(shape, 0) % KINDS == index // (2 * count))
+        return jnp.where(hit, 1.0, 0.0).astype(bf16)
+
+    cut = KINDS * rows
+    bx_out[:cut, :] = boxes(rows, own_place)
+    bx_out[cut : cut + KINDS * block, :] = boxes(block, other_place)
+    bx_out[cut + KINDS * block :, :] = boxes(block, lambda index: other_place(index + block))
+    br_out[...] = row_boxes(rows, own_place)
+    bt_out[...] = row_boxes(block, own_place)
+    bl_out[...] = row_boxes(block, lambda index: own_place(index + block))
     high, low = split(inside(own_offset, bands))
     rh_out[:, :rows] = high
     rl_out[:, :rows] = low
@@ -271,13 +281,13 @@
 
 
 def finish_kernel(
-    sc, other, td, to, hd, er, ec, eo, q, kc0, kc1,
+    other, td, to, hd, er, ec, eo, q, kc0, kc1,
     td_out, to_out, hd_out, h0_out, h1_out, q_out,
 ):
     rows = other.shape[0]
     block = rows // 2
     twice = q.shape[0]
-    own_place, other_place, fade = edge_tools(sc, rows, block)
+    own_place, other_place, fade = edge_tools(position()[1] == 0, rows, block)
     shape = (rows, twice)
     own_column = fade(own_place(iota(shape, 0)), shape, 1)
     other_column = fade(other_place(iota(shape, 0)), shape, 1)
@@ -324,10 +334,10 @@
 def contract_kernel(peer_counts, slots, scale, owners, info, *refs):
     count = len(peer_counts)
     packs = refs[:count]
-    td, to, hd, h0, h1, q, bd, b0, b1, br, rh, rl, out, m_box, final = refs[count:]
+    td, to, hd, h0, h1, q, bx, br, bt, bl, rh, rl, out, final = refs[count:]
     rows = td.shape[1]
     block = rows // 2
-    bands = bd.shape[1]
+    bands = bx.shape[1]
     twice = 2 * bands
     own = info[...]
     total = extra = 0.0
@@ -361,52 +371,53 @@
     pair0 = jnp.concatenate([s_c0, s_c0], axis=1)
     pair1 = jnp.concatenate([s_c1, s_c1], axis=1)
 
-    def boxed(x, box):
-        high, low = split(x)
-        return dot(high, box) + dot(low, box)
-
-    for kind in range(KINDS):
-        top, mid, end = kind * rows, kind * rows + block, (kind + 1) * rows
-        acc = jnp.zeros((rows, bands), f32)
-        acc_top = jnp.zeros((block, bands), f32)
-        acc_low = jnp.zeros((block, bands), f32)
-        for second in range(kind, KINDS):
-            here = slice(second * rows, (second + 1) * rows)
+    def parts(values):
+        return jnp.concatenate([part for value in values for part in split(value)], axis=0)
+
+    pieces = range(0, KINDS * block, rows)
+    sums = []
+    for second in range(KINDS):
+        products = []
+        for kind in range(second + 1):
             at = pair_index(kind, second) * rows
             value = half_own if second == kind else s_own
-            acc = acc + boxed(value * td[at : at + rows, :], bd[here, :])
-        for second in range(0, KINDS, 2):
-            here = slice(second * block, (second + 2) * block)
-            acc_top = acc_top + boxed(pair0 * to[top:mid, here], b0[here, :])
-            acc_low = acc_low + boxed(pair1 * to[mid:end, here], b1[here, :])
-        m_box[top:mid, :] = acc[:block] + acc_top
-        m_box[mid:end, :] = acc[block:] + acc_low
-    high, low = split(m_box[...])
-    result = dot(br[...], high) + dot(br[...], low)
-
-    reach = (rh[:, :rows], rl[:, :rows])
-    reach0 = (rh[:, :block], rl[:, :block])
-    reach1 = (rh[:, block:rows], rl[:, block:rows])
-    over0 = (rh[:, rows : rows + block], rl[:, rows : rows + block])
-    over1 = (rh[:, rows + block :], rl[:, rows + block :])
-
-    def three(a, b, multiply):
-        return multiply(a[0], b[0]) + multiply(a[0], b[1]) + multiply(a[1], b[0])
-
-    part_own, part0, part1 = split(s_own), split(s_c0), split(s_c1)
-    y_own = three(reach, part_own, dot)
-    y_off = jnp.concatenate([three(over0, part0, dot_t), three(over1, part1, dot_t)], axis=1)
-    y_0 = three(reach0, part0, dot)
-    y_1 = three(reach1, part1, dot)
-    fourth = three(split(0.5 * y_own + y_off), reach, dot_t) * q[...]
+            products.append(value * td[at : at + rows, :])
+        sums.append(dot(br[:, : 2 * rows * (second + 1)], parts(products)))
+    starts = range(0, KINDS * rows, rows)
+    for at in pieces:
+        products = [pair0 * to[top : top + block, at : at + rows] for top in starts]
+        sums.append(dot(bt[...], parts(products)))
+    for at in pieces:
+        products = [pair1 * to[top + block : top + rows, at : at + rows] for top in starts]
+        sums.append(dot(bl[...], parts(products)))
+
+    def reach(at):
+        return jnp.concatenate([rh[:, at], rl[:, at], rh[:, at]], axis=1)
+
+    def thrice(x, axis):
+        high, low = split(x)
+        return jnp.concatenate([high, high, low], axis=axis)
+
+    own_at = slice(0, rows)
+    at0, at1 = slice(0, block), slice(block, rows)
+    over0, over1 = slice(rows, rows + block), slice(rows + block, 2 * rows)
+    y_own = dot(reach(own_at), thrice(s_own, 0))
+    y_off = jnp.concatenate(
+        [dot_t(reach(over0), thrice(s_c0, 1)), dot_t(reach(over1), thrice(s_c1, 1))], axis=1
+    )
+    y_0 = dot(reach(at0), thrice(s_c0, 0))
+    y_1 = dot(reach(at1), thrice(s_c1, 0))
+    fourth = dot_t(reach(own_at), thrice(0.5 * y_own + y_off, 1)) * q[...]
     y_own = y_own + y_off
-    second = jnp.zeros((twice, bands), f32)
-    for kind in range(KINDS):
-        here = slice(kind * rows, (kind + 1) * rows)
-        second = second + boxed(y_own * hd[:, here], bd[here, :])
-        here = slice(kind * block, (kind + 1) * block)
-        second = second + boxed(y_0 * h0[:, here], b0[here, :])
-        second = second + boxed(y_1 * h1[:, here], b1[here, :])
+    y_0 = jnp.concatenate([y_0, y_0], axis=1)
+    y_1 = jnp.concatenate([y_1, y_1], axis=1)
+    edges = [y_own * hd[:, at : at + rows] for at in starts]
+    edges += [y_0 * h0[:, at : at + rows] for at in pieces]
+    edges += [y_1 * h1[:, at : at + rows] for at in pieces]
+    both = parts([jnp.concatenate(sums, axis=1), jnp.concatenate(edges, axis=1)])
+    both = dot(both, bx[...])
+    result = both[:bands] + both[bands:twice]
+    second = both[twice : 2 * twice] + both[2 * twice :]
     fourth = fourth[:bands] + fourth[bands:]
     result = result - second[:bands] - second[bands:] + fourth[:, :bands] + fourth[:, bands:]
     final[...] = jnp.zeros(final.shape, f32)
@@ -473,13 +484,10 @@
     bands = band_starts.shape[1]
     twice = 2 * bands
     groups, owners = lax.axis_size("bl"), lax.axis_size("bp")
-    per_half = owners // 2
     assert local_count == 1 and width == 2 * rows and block == 128 == twice
-    owner, group = lax.axis_index("bp"), lax.axis_index("bl")
-    sc = jnp.stack([owner // per_half, owner % per_half, owner, group]).astype(jnp.int32)
     panel, diag, info, pack = pl.pallas_call(
         pack_kernel,
-        in_specs=[SMEM, HBM, HBM, HBM, HBM],
+        in_specs=[HBM] * 4,
         out_specs=[VMEM] * 4,
         out_shape=[
             jax.ShapeDtypeStruct((rows, width), f32),
@@ -490,13 +498,12 @@
         scratch_shapes=[
             pltpu.VMEM((rows, width), f32),
             pltpu.VMEM((1, channels), jnp.int32),
-            pltpu.SMEM(partner_ids.shape, jnp.int32),
+            pltpu.VMEM(partner_ids.shape, jnp.int32),
             pltpu.VMEM(band_starts.shape, jnp.int32),
             pltpu.SemaphoreType.DMA((4,)),
         ],
         compiler_params=params(16),
     )(
-        sc,
         in_hbm(inverse_cov),
         in_hbm(channel_keep_mask),
         in_hbm(partner_ids),
@@ -519,16 +526,16 @@
         ((twice, twice), f32),
         ((3 * rows, KINDS * block), bf16),
         ((3 * rows, KINDS * block), bf16),
-        ((KINDS * rows, bands), bf16),
-        ((KINDS * block, bands), bf16),
-        ((KINDS * block, bands), bf16),
-        ((bands, KINDS * rows), bf16),
+        ((2 * KINDS * rows, bands), bf16),
+        ((bands, 2 * KINDS * rows), bf16),
+        ((bands, 2 * KINDS * block), bf16),
+        ((bands, 2 * KINDS * block), bf16),
         ((twice, width), bf16),
         ((twice, width), bf16),
     ]
     begun = pl.pallas_call(
         prepare_kernel,
-        in_specs=[SMEM, VMEM, VMEM],
+        in_specs=[VMEM, VMEM],
         out_specs=[VMEM] * len(shapes),
         out_shape=[jax.ShapeDtypeStruct(shape, kind) for shape, kind in shapes],
         scratch_shapes=[
@@ -540,7 +547,7 @@
         cost_estimate=pl.CostEstimate(
             flops=4_000_000_000, bytes_accessed=8 << 20, transcendentals=1 << 20
         ),
-    )(sc, info, panel)
+    )(info, panel)
     ends = shapes[:2] + [
         ((twice, KINDS * rows), f32),
         ((twice, KINDS * block), f32),
@@ -549,15 +556,15 @@
     ]
     tables = pl.pallas_call(
         finish_kernel,
-        in_specs=[SMEM] + [VMEM] * 10,
+        in_specs=[VMEM] * 10,
         out_specs=[VMEM] * len(ends),
         out_shape=[jax.ShapeDtypeStruct(shape, kind) for shape, kind in ends],
-        input_output_aliases={2: 0, 3: 1},
+        input_output_aliases={1: 0, 2: 1},
         compiler_params=params(16),
         cost_estimate=pl.CostEstimate(
             flops=2_000_000_000, bytes_accessed=8 << 20, transcendentals=1 << 17
         ),
-    )(sc, other, *begun[:9])
+    )(other, *begun[:9])
     tables = [*tables, *begun[9:]]
 
     scale = 1.0 / (4 * local_count * groups * WINDOW)
@@ -569,10 +576,7 @@
         in_specs=[VMEM] * (1 + len(arrived) + len(tables)),
         out_specs=VMEM,
         out_shape=jax.ShapeDtypeStruct((groups * owners, 1, block), f32),
-        scratch_shapes=[
-            pltpu.VMEM((KINDS * rows, bands), f32),
-            pltpu.VMEM((twice, twice), f32),
-        ],
+        scratch_shapes=[pltpu.VMEM((twice, twice), f32)],
         compiler_params=params(30),
     )(info, *arrived, *tables)
 

time: 34.7 us -> 33.6 us (0.968)
  Pallas kernels: 13.4 us -> 11.7 us
  waiting for transfers between devices: 1.85 us -> 2.54 us
    pallas_call x3, Pallas kernels: 9.88 us -> 8.64 us  [the longest x1 5.68 us: body(): pl.pallas_call(prepare_kernel, in_specs=[VMEM, VMEM], out_specs=[VMEM] *...]
    ppermute x4, waiting for transfers between devices: 0.58 us -> 1.08 us  [body(): arrived = [lax.ppermute(pack, 'bl', route) for route, _ in routes]]
    pallas_call x1, Pallas kernels: 2.8 us -> 2.33 us  [body(): pl.pallas_call(partial(contract_kernel, [both for _, both in routes], par...]
  transfers between devices with their start and end apart: 5 -> 5, of which waited for: 2 -> 3; matrix products, arithmetic and copies ran while one was open for 0% -> 0% of each run, Pallas kernels for 23% -> 22%
where the time goes in v4:
time: 33.6 us; the launch traced here: 33.5 us
  blocking collectives  13.1 us (39%)
  Pallas kernels  11.7 us (35%)
  starting transfers between devices  6.18 us (18%)
  waiting for transfers between devices  2.54 us (8%)
    all_to_all x1, blocking collectives, body(): met = lax.all_to_all(parts, ('bl', 'bp'), 0, 0, tiled=True)  13.1 us
    pallas_call x1, Pallas kernels, body(): pl.pallas_call(prepare_kernel, in_specs=[VMEM, VMEM], out_specs=[VMEM] *...  5.68 us
    ppermute x4, starting transfers between devices, body(): arrived = [lax.ppermute(pack, 'bl', route) for route, _ in routes]  4.61 us
    pallas_call x1, Pallas kernels, body(): pl.pallas_call(partial(contract_kernel, [both for _, both in routes], par...  2.33 us
    pallas_call x1, Pallas kernels, body(): pl.pallas_call(finish_kernel, in_specs=[VMEM] * 10, out_specs=[VMEM] * le...  1.65 us
    ppermute x1, starting transfers between devices, body(): lax.ppermute(diag, 'bp', [(place, place ^ 1) for place in range(owners)])  1.58 us
    ppermute x1, waiting for transfers between devices, body(): lax.ppermute(diag, 'bp', [(place, place ^ 1) for place in range(owners)])  1.45 us
    pallas_call x1, Pallas kernels, body(): pl.pallas_call(pack_kernel, in_specs=[HBM] * 4, out_specs=[VMEM] * 4, out...  1.31 us
  transfers between devices with their start and end apart: 5, of which 3 were waited for; matrix products, arithmetic and copies ran while one was open for 0% of the time, Pallas kernels for 22%

profile of v4, /device:TPU:0, one launch (start us, length us, event | category | flops | bytes accessed | tf_op | source)
XLA Modules:
  0.0 33.5 jit_solution(16356467474211904366)
XLA Ops:
  0.0 1.3 %shard_map.46 = (f32[256,512]{1,0:T(8,128)S(1)}, f32[256,256]{1,0:T(8,128)S(1)}, f32[8,128]{1,0:T(8,128)S(1)}, f32[520,128]{1,0:T(8,128)S(1)}) custom-call(f32[1,256,1024]{2,1,0:T(8,128)} %cov_hbm.1, s32[1,1024]{1,0:T(1,128)} %keep_hbm.1, s32[1,2]{1,0:T(1,128)} %pid_hbm.1, s32[2,64]{1,0:T(2,128)} %starts_hbm.1), custom_call_target="tpu_custom_call" | custom-call | tf_op jit(solution)/shard_map/pallas_call | solution.py:488
  1.3 4.0 %collective-permute-start = (f32[520,128]{1,0:T(8,128)S(1)}, f32[520,128]{1,0:T(8,128)S(1)}, u32[]{:S(2)}, u32[]{:S(2)}) collective-permute-start(f32[520,128]{1,0:T(8,128)S(1)} %get-tuple-element.31), channel_id=1, source_target_pairs={{0,24},{4,28},{8,16},{12,20},{16,12},{20,8},{24,4},{28,0},{1,25},{... | collective-permute-start | bytes 798728 | tf_op jit(solution)/shard_map/ppermute | solution.py:515
  5.3 0.5 %collective-permute-start.1 = (f32[520,128]{1,0:T(8,128)S(1)}, f32[520,128]{1,0:T(8,128)S(1)}, u32[]{:S(2)}, u32[]{:S(2)}) collective-permute-start(f32[520,128]{1,0:T(8,128)S(1)} %get-tuple-element.31), channel_id=1, source_target_pairs={{0,8},{4,12},{8,4},{12,0},{16,24},{20,28},{24,20},{28,16},{1,9},{5... | collective-permute-start | bytes 798728 | tf_op jit(solution)/shard_map/ppermute | solution.py:515
  5.8 0.1 collective-permute-start.2
  5.9 0.0 collective-permute-start.3
  5.9 1.6 %collective-permute-start.4 = (f32[256,256]{1,0:T(8,128)S(1)}, f32[256,256]{1,0:T(8,128)S(1)}, u32[]{:S(2)}, u32[]{:S(2)}) collective-permute-start(f32[256,256]{1,0:T(8,128)S(1)} %get-tuple-element.32), channel_id=1, source_target_pairs={{0,1},{1,0},{2,3},{3,2},{4,5},{5,4},{6,7},{7,6},{8,9},{9,8},{10,11... | collective-permute-start | bytes 786440 | tf_op jit(solution)/shard_map/ppermute | solution.py:513
  7.5 5.7 %shard_map.47 = (f32[2560,256]{1,0:T(8,128)S(1)}, f32[1024,512]{1,0:T(8,128)S(1)}, f32[144,1024]{1,0:T(8,128)S(1)}, f32[144,128]{1,0:T(8,128)S(1)}, f32[144,256]...) custom-call(f32[8,128]{1,0:T(8,128)S(1)} %get-tuple-element.30.info,, ...), custom_call_target="tpu_custom_call" | custom-call | flops 4000000000 | bytes 8388608 | tf_op jit(solution)/shard_map/pallas_call | solution.py:536
  13.2 1.5 %collective-permute-done.4.other = f32[256,256]{1,0:T(8,128)S(1)} collective-permute-done((f32[256,256]{1,0:T(8,128)S(1)}, f32[256,256]{1,0:T(8,128)S(1)}, u32[]{:S(2)}, u32[]{:S(2)}) %collective-permute-start.4) | collective-permute-done | bytes 262176 | tf_op jit(solution)/shard_map/ppermute | solution.py:513
  14.6 1.6 %shard_map.48 = (f32[2560,256]{1,0:T(8,128)S(1)}, f32[1024,512]{1,0:T(8,128)S(1)}, f32[128,1024]{1,0:T(8,128)S(1)}, f32[128,512]{1,0:T(8,128)S(1)}, f32[128,512]{1,0:T(8,128)S(1)}, /*index=5*/f32[128,128]{1,0:T(8,128)S(1)}) custom-call(f32[256,256]{1,0:T(8,128)S(1)} %collective-permute-done.4.other, ...), custom_call_target="tpu_custom_call", output_to_operand_aliasing={{0}: (1, {}), {1}: (2, {})} | custom-call | flops 2000000000 | bytes 8388608 | tf_op jit(solution)/shard_map/pallas_call | solution.py:557
  16.3 0.0 collective-permute-done.refs_0_
  16.3 0.4 %collective-permute-done.1.refs_1_ = f32[520,128]{1,0:T(8,128)S(1)} collective-permute-done((f32[520,128]{1,0:T(8,128)S(1)}, f32[520,128]{1,0:T(8,128)S(1)}, u32[]{:S(2)}, u32[]{:S(2)}) %collective-permute-start.1) | collective-permute-done | bytes 266272 | tf_op jit(solution)/shard_map/ppermute | solution.py:515
  16.7 0.7 %collective-permute-done.2.refs_2_ = f32[520,128]{1,0:T(8,128)S(1)} collective-permute-done((f32[520,128]{1,0:T(8,128)S(1)}, f32[520,128]{1,0:T(8,128)S(1)}, u32[]{:S(2)}, u32[]{:S(2)}) %collective-permute-start.2) | collective-permute-done | bytes 266272 | tf_op jit(solution)/shard_map/ppermute | solution.py:515
  17.4 0.0 collective-permute-done.3.refs_3_
  17.4 2.3 %shard_map.49 = f32[32,1,128]{2,1,0:T(1,128)S(1)} custom-call(f32[8,128]{1,0:T(8,128)S(1)} %get-tuple-element.30.info, f32[520,128]{1,0:T(8,128)S(1)} %collective-permute-done.refs_0_, f32[520,128]{1,0:T(8,128)S(1)} %collective-permute-done.1.refs_1_, f32[520,128]{1,0:T(8,128)S(1)} %collective-permute-done.2.refs_2_, ...), custom_call_target="tpu_custom_call" | custom-call | tf_op jit(solution)/shard_map/pallas_call | solution.py:572
  19.7 13.1 %all_to_all.5.parts = f32[32,1,128]{2,1,0:T(1,128)S(1)} all-to-all(f32[32,1,128]{2,1,0:T(1,128)S(1)} %shard_map.49), channel_id=1, replica_groups=mesh['bl'=8,'bp'=4] {'bl','bp'}, dimensions={0} | all-to-all | bytes 32768 | tf_op jit(solution)/shard_map/all_to_all | solution.py:583
  32.8 0.7 %shard_map.50 = f32[2,8,16]{2,1,0:T(8,128)} custom-call(f32[32,1,128]{2,1,0:T(1,128)S(1)} %all_to_all.5.parts), custom_call_target="tpu_custom_call" | custom-call | tf_op jit(solution)/shard_map/pallas_call | solution.py:584
Async XLA Ops:
  1.3 15.0 %collective-permute-start = (f32[520,128]{1,0:T(8,128)S(1)}, f32[520,128]{1,0:T(8,128)S(1)}, u32[]{:S(2)}, u32[]{:S(2)}) collective-permute-start(f32[520,128]{1,0:T(8,128)S(1)} %get-tuple-element.31), channel_id=1, source_target_pairs={{0,24},{4,28},{8,16},{12,20},{16,12},{20,8},{24,4},{28,0},{1,25},{... | collective-permute-start | bytes 798728 | tf_op jit(solution)/shard_map/ppermute | solution.py:515
  5.3 11.4 %collective-permute-start.1 = (f32[520,128]{1,0:T(8,128)S(1)}, f32[520,128]{1,0:T(8,128)S(1)}, u32[]{:S(2)}, u32[]{:S(2)}) collective-permute-start(f32[520,128]{1,0:T(8,128)S(1)} %get-tuple-element.31), channel_id=1, source_target_pairs={{0,8},{4,12},{8,4},{12,0},{16,24},{20,28},{24,20},{28,16},{1,9},{5... | collective-permute-start | bytes 798728 | tf_op jit(solution)/shard_map/ppermute | solution.py:515
  5.8 11.6 %collective-permute-start.2 = (f32[520,128]{1,0:T(8,128)S(1)}, f32[520,128]{1,0:T(8,128)S(1)}, u32[]{:S(2)}, u32[]{:S(2)}) collective-permute-start(f32[520,128]{1,0:T(8,128)S(1)} %get-tuple-element.31), channel_id=1, source_target_pairs={{0,16},{4,20},{8,24},{12,28},{16,4},{20,0},{24,12},{28,8},{1,17},{... | collective-permute-start | bytes 798728 | tf_op jit(solution)/shard_map/ppermute | solution.py:515
  5.9 11.5 %collective-permute-start.3 = (f32[520,128]{1,0:T(8,128)S(1)}, f32[520,128]{1,0:T(8,128)S(1)}, u32[]{:S(2)}, u32[]{:S(2)}) collective-permute-start(f32[520,128]{1,0:T(8,128)S(1)} %get-tuple-element.31), channel_id=1, source_target_pairs={{0,4},{4,0},{8,12},{12,8},{16,20},{20,16},{24,28},{28,24},{1,5},{5... | collective-permute-start | bytes 798728 | tf_op jit(solution)/shard_map/ppermute | solution.py:515
  5.9 8.7 %collective-permute-start.4 = (f32[256,256]{1,0:T(8,128)S(1)}, f32[256,256]{1,0:T(8,128)S(1)}, u32[]{:S(2)}, u32[]{:S(2)}) collective-permute-start(f32[256,256]{1,0:T(8,128)S(1)} %get-tuple-element.32), channel_id=1, source_target_pairs={{0,1},{1,0},{2,3},{3,2},{4,5},{5,4},{6,7},{7,6},{8,9},{9,8},{10,11... | collective-permute-start | bytes 786440 | tf_op jit(solution)/shard_map/ppermute | solution.py:513

commit v5 on v4

--- a/solution.py
+++ b/solution.py
@@ -462,7 +462,7 @@
             def target(source, step=step):
                 team, member = divmod(source, 2)
                 goal = team ^ step
-                return goal * 2 + (member if team < goal else 1 - member)
+                return goal * 2 + (member if (team < goal) == (step == 3) else 1 - member)
 
             routes.append(([(source, target(source)) for source in range(groups)], True))
         routes.append(([(source, source ^ 1) for source in range(groups)], False))

time: 33.6 us -> 33.6 us (level)
  blocking collectives: 13.1 us -> 12.7 us
    ppermute x4, waiting for transfers between devices: 1.08 us -> 1.66 us  [body(): arrived = [lax.ppermute(pack, 'bl', route) for route, _ in routes]]
    ppermute x1, waiting for transfers between devices: 1.45 us -> 0.93 us  [body(): lax.ppermute(diag, 'bp', [(place, place ^ 1) for place in range(owners)])]
    all_to_all x1, blocking collectives: 13.1 us -> 12.7 us  [body(): met = lax.all_to_all(parts, ('bl', 'bp'), 0, 0, tiled=True)]
  transfers between devices with their start and end apart: 5 -> 5, of which waited for: 3 -> 2; matrix products, arithmetic and copies ran while one was open for 0% -> 0% of each run, Pallas kernels for 22% -> 22%
where the time goes in v5:
time: 33.6 us; the launch traced here: 33.4 us
  blocking collectives  12.7 us (38%)
  Pallas kernels  11.7 us (35%)
  starting transfers between devices  6.43 us (19%)
  waiting for transfers between devices  2.59 us (8%)
    all_to_all x1, blocking collectives, body(): met = lax.all_to_all(parts, ('bl', 'bp'), 0, 0, tiled=True)  12.7 us
    pallas_call x1, Pallas kernels, body(): pl.pallas_call(prepare_kernel, in_specs=[VMEM, VMEM], out_specs=[VMEM] *...  5.68 us
    ppermute x4, starting transfers between devices, body(): arrived = [lax.ppermute(pack, 'bl', route) for route, _ in routes]  4.63 us
    pallas_call x1, Pallas kernels, body(): pl.pallas_call(partial(contract_kernel, [both for _, both in routes], par...  2.33 us
    ppermute x1, starting transfers between devices, body(): lax.ppermute(diag, 'bp', [(place, place ^ 1) for place in range(owners)])  1.8 us
    ppermute x4, waiting for transfers between devices, body(): arrived = [lax.ppermute(pack, 'bl', route) for route, _ in routes]  1.66 us
    pallas_call x1, Pallas kernels, body(): pl.pallas_call(finish_kernel, in_specs=[VMEM] * 10, out_specs=[VMEM] * le...  1.65 us
    pallas_call x1, Pallas kernels, body(): pl.pallas_call(pack_kernel, in_specs=[HBM] * 4, out_specs=[VMEM] * 4, out...  1.31 us
  transfers between devices with their start and end apart: 5, of which 2 were waited for; matrix products, arithmetic and copies ran while one was open for 0% of the time, Pallas kernels for 22%

profile of v5, /device:TPU:0, one launch (start us, length us, event | category | flops | bytes accessed | tf_op | source)
XLA Modules:
  0.0 33.4 jit_solution(9744151873366320404)
XLA Ops:
  0.0 1.3 %shard_map.46 = (f32[256,512]{1,0:T(8,128)S(1)}, f32[256,256]{1,0:T(8,128)S(1)}, f32[8,128]{1,0:T(8,128)S(1)}, f32[520,128]{1,0:T(8,128)S(1)}) custom-call(f32[1,256,1024]{2,1,0:T(8,128)} %cov_hbm.1, s32[1,1024]{1,0:T(1,128)} %keep_hbm.1, s32[1,2]{1,0:T(1,128)} %pid_hbm.1, s32[2,64]{1,0:T(2,128)} %starts_hbm.1), custom_call_target="tpu_custom_call" | custom-call | tf_op jit(solution)/shard_map/pallas_call | solution.py:488
  1.3 4.0 %collective-permute-start = (f32[520,128]{1,0:T(8,128)S(1)}, f32[520,128]{1,0:T(8,128)S(1)}, u32[]{:S(2)}, u32[]{:S(2)}) collective-permute-start(f32[520,128]{1,0:T(8,128)S(1)} %get-tuple-element.31), channel_id=1, source_target_pairs={{0,24},{4,28},{8,16},{12,20},{16,12},{20,8},{24,4},{28,0},{1,25},{... | collective-permute-start | bytes 798728 | tf_op jit(solution)/shard_map/ppermute | solution.py:515
  5.3 0.0 collective-permute-start.1
  5.3 0.3 %collective-permute-start.2 = (f32[520,128]{1,0:T(8,128)S(1)}, f32[520,128]{1,0:T(8,128)S(1)}, u32[]{:S(2)}, u32[]{:S(2)}) collective-permute-start(f32[520,128]{1,0:T(8,128)S(1)} %get-tuple-element.31), channel_id=1, source_target_pairs={{0,20},{4,16},{8,28},{12,24},{16,0},{20,4},{24,8},{28,12},{1,21},{... | collective-permute-start | bytes 798728 | tf_op jit(solution)/shard_map/ppermute | solution.py:515
  5.6 0.3 collective-permute-start.3
  6.0 1.8 %collective-permute-start.4 = (f32[256,256]{1,0:T(8,128)S(1)}, f32[256,256]{1,0:T(8,128)S(1)}, u32[]{:S(2)}, u32[]{:S(2)}) collective-permute-start(f32[256,256]{1,0:T(8,128)S(1)} %get-tuple-element.32), channel_id=1, source_target_pairs={{0,1},{1,0},{2,3},{3,2},{4,5},{5,4},{6,7},{7,6},{8,9},{9,8},{10,11... | collective-permute-start | bytes 786440 | tf_op jit(solution)/shard_map/ppermute | solution.py:513
  7.8 5.7 %shard_map.47 = (f32[2560,256]{1,0:T(8,128)S(1)}, f32[1024,512]{1,0:T(8,128)S(1)}, f32[144,1024]{1,0:T(8,128)S(1)}, f32[144,128]{1,0:T(8,128)S(1)}, f32[144,256]...) custom-call(f32[8,128]{1,0:T(8,128)S(1)} %get-tuple-element.30.info,, ...), custom_call_target="tpu_custom_call" | custom-call | flops 4000000000 | bytes 8388608 | tf_op jit(solution)/shard_map/pallas_call | solution.py:536
  13.4 0.9 %collective-permute-done.4.other = f32[256,256]{1,0:T(8,128)S(1)} collective-permute-done((f32[256,256]{1,0:T(8,128)S(1)}, f32[256,256]{1,0:T(8,128)S(1)}, u32[]{:S(2)}, u32[]{:S(2)}) %collective-permute-start.4) | collective-permute-done | bytes 262176 | tf_op jit(solution)/shard_map/ppermute | solution.py:513
  14.4 1.6 %shard_map.48 = (f32[2560,256]{1,0:T(8,128)S(1)}, f32[1024,512]{1,0:T(8,128)S(1)}, f32[128,1024]{1,0:T(8,128)S(1)}, f32[128,512]{1,0:T(8,128)S(1)}, f32[128,512]{1,0:T(8,128)S(1)}, /*index=5*/f32[128,128]{1,0:T(8,128)S(1)}) custom-call(f32[256,256]{1,0:T(8,128)S(1)} %collective-permute-done.4.other, ...), custom_call_target="tpu_custom_call", output_to_operand_aliasing={{0}: (1, {}), {1}: (2, {})} | custom-call | flops 2000000000 | bytes 8388608 | tf_op jit(solution)/shard_map/pallas_call | solution.py:557
  16.0 0.0 collective-permute-done.refs_0_
  16.0 1.7 %collective-permute-done.1.refs_1_ = f32[520,128]{1,0:T(8,128)S(1)} collective-permute-done((f32[520,128]{1,0:T(8,128)S(1)}, f32[520,128]{1,0:T(8,128)S(1)}, u32[]{:S(2)}, u32[]{:S(2)}) %collective-permute-start.1) | collective-permute-done | bytes 266272 | tf_op jit(solution)/shard_map/ppermute | solution.py:515
  17.7 0.0 collective-permute-done.2.refs_2_
  17.7 0.0 collective-permute-done.3.refs_3_
  17.7 2.3 %shard_map.49 = f32[32,1,128]{2,1,0:T(1,128)S(1)} custom-call(f32[8,128]{1,0:T(8,128)S(1)} %get-tuple-element.30.info, f32[520,128]{1,0:T(8,128)S(1)} %collective-permute-done.refs_0_, f32[520,128]{1,0:T(8,128)S(1)} %collective-permute-done.1.refs_1_, f32[520,128]{1,0:T(8,128)S(1)} %collective-permute-done.2.refs_2_, ...), custom_call_target="tpu_custom_call" | custom-call | tf_op jit(solution)/shard_map/pallas_call | solution.py:572
  20.0 12.7 %all_to_all.5.parts = f32[32,1,128]{2,1,0:T(1,128)S(1)} all-to-all(f32[32,1,128]{2,1,0:T(1,128)S(1)} %shard_map.49), channel_id=1, replica_groups=mesh['bl'=8,'bp'=4] {'bl','bp'}, dimensions={0} | all-to-all | bytes 32768 | tf_op jit(solution)/shard_map/all_to_all | solution.py:583
  32.7 0.7 %shard_map.50 = f32[2,8,16]{2,1,0:T(8,128)} custom-call(f32[32,1,128]{2,1,0:T(1,128)S(1)} %all_to_all.5.parts), custom_call_target="tpu_custom_call" | custom-call | tf_op jit(solution)/shard_map/pallas_call | solution.py:584
Async XLA Ops:
  1.3 14.7 %collective-permute-start = (f32[520,128]{1,0:T(8,128)S(1)}, f32[520,128]{1,0:T(8,128)S(1)}, u32[]{:S(2)}, u32[]{:S(2)}) collective-permute-start(f32[520,128]{1,0:T(8,128)S(1)} %get-tuple-element.31), channel_id=1, source_target_pairs={{0,24},{4,28},{8,16},{12,20},{16,12},{20,8},{24,4},{28,0},{1,25},{... | collective-permute-start | bytes 798728 | tf_op jit(solution)/shard_map/ppermute | solution.py:515
  5.3 12.4 %collective-permute-start.1 = (f32[520,128]{1,0:T(8,128)S(1)}, f32[520,128]{1,0:T(8,128)S(1)}, u32[]{:S(2)}, u32[]{:S(2)}) collective-permute-start(f32[520,128]{1,0:T(8,128)S(1)} %get-tuple-element.31), channel_id=1, source_target_pairs={{0,12},{4,8},{8,0},{12,4},{16,28},{20,24},{24,16},{28,20},{1,13},{... | collective-permute-start | bytes 798728 | tf_op jit(solution)/shard_map/ppermute | solution.py:515
  5.3 12.4 %collective-permute-start.2 = (f32[520,128]{1,0:T(8,128)S(1)}, f32[520,128]{1,0:T(8,128)S(1)}, u32[]{:S(2)}, u32[]{:S(2)}) collective-permute-start(f32[520,128]{1,0:T(8,128)S(1)} %get-tuple-element.31), channel_id=1, source_target_pairs={{0,20},{4,16},{8,28},{12,24},{16,0},{20,4},{24,8},{28,12},{1,21},{... | collective-permute-start | bytes 798728 | tf_op jit(solution)/shard_map/ppermute | solution.py:515
  5.6 12.0 %collective-permute-start.3 = (f32[520,128]{1,0:T(8,128)S(1)}, f32[520,128]{1,0:T(8,128)S(1)}, u32[]{:S(2)}, u32[]{:S(2)}) collective-permute-start(f32[520,128]{1,0:T(8,128)S(1)} %get-tuple-element.31), channel_id=1, source_target_pairs={{0,4},{4,0},{8,12},{12,8},{16,20},{20,16},{24,28},{28,24},{1,5},{5... | collective-permute-start | bytes 798728 | tf_op jit(solution)/shard_map/ppermute | solution.py:515
  6.0 8.4 %collective-permute-start.4 = (f32[256,256]{1,0:T(8,128)S(1)}, f32[256,256]{1,0:T(8,128)S(1)}, u32[]{:S(2)}, u32[]{:S(2)}) collective-permute-start(f32[256,256]{1,0:T(8,128)S(1)} %get-tuple-element.32), channel_id=1, source_target_pairs={{0,1},{1,0},{2,3},{3,2},{4,5},{5,4},{6,7},{7,6},{8,9},{9,8},{10,11... | collective-permute-start | bytes 786440 | tf_op jit(solution)/shard_map/ppermute | solution.py:513
